TPU v7x, 32 devices: a whole 2x2x4 slice. The times are simulated.
32 devices in a mesh: cluster: 4 (over z), tm: 8 (over y, x, core).
Axes of the slice: x: 2, y: 2, z: 4, core: 2. Of those that a mesh axis runs over, the one named last changes fastest.
Arguments:
- obs: float32 [12, 512, 128], P('cluster', 'tm'), parts along dimension 0, may hold values from -6 to 6
- present: int32 [12, 512], P('cluster', 'tm'), parts along dimension 0, may hold values 0 or 1
- sensors: int32 [4], P('cluster'), parts along dimension 0, may hold values from 32 to 128
- log_prec: float32 [512], P('cluster'), parts along dimension 0, may hold values from -1 to 1
- dynamics: float32 [512, 128], P('cluster'), parts along dimension 0, may hold values from -1 to 1
- prior_var: float32 [512], P('cluster'), parts along dimension 0, may hold values from 0 to 0.06, as said below
- obs_map: float32 [512, 128], P('cluster'), parts along dimension 0, may hold values from -0.5 to 0.5
- init_state: float32 [12, 128], P('cluster'), parts along dimension 0, may hold values from -6 to 6
Outputs:
- smoothed: float32 [12, 512, 128], P('cluster', 'tm'), parts along dimension 0
- new_log_prec: float32 [512], P('cluster'), parts along dimension 0
- mean_loglik: float32 [4], P('cluster'), parts along dimension 0
There are 4 independent parts, one for each index of `cluster`. A program takes and returns all parts, laid end to end along the dimension named above; each array names one. Nothing has to cross between parts.
Inputs may be any that keep to these rules, and one draw needn't show every extreme that they name: `prior_var`: positive variances.
All inputs are finite; a program needn't handle non-finite values. No bound on the sum of `present` on one device may be relied on, other than what follows from the above.
Results may differ from a plain program's by a relative error of at most 0.0003.
Values sent between devices are 32-bit elements; how exact they have to be, the bound alone decides.
A program may use at most 128 MiB of HBM per device.

v0:
```python
import functools
import math

import jax
import jax.numpy as jnp
from jax import lax
from jax.experimental import pallas as pl
from jax.experimental.pallas import tpu as pltpu
from jax.sharding import PartitionSpec as P

F32 = jnp.float32
BF16 = jnp.bfloat16
MESH = pl.DeviceIdType.MESH
WORD = 4


def stacked(a):
    high = a.astype(BF16).astype(F32)
    return jnp.concatenate([high, a - high], axis=0).astype(BF16)


def twice(s):
    return jnp.concatenate([s, s], axis=1)


def product(left, right):
    full = jnp.dot(left, right, preferred_element_type=F32)
    rows = full.shape[0] // 2
    return full[:rows] + full[rows:]


def times(a, right):
    return product(twice(stacked(a)), right)


def over(count, width, body):
    if count <= width:
        for i in range(count):
            body(i)
        return
    assert count % width == 0

    def step(lap, _):
        for i in range(width):
            body(lap * width + i)
        return 0

    lax.fori_loop(0, count // width, step, 0)


def kernel(
    n, seqs, steps,
    present_s, sensors_s, obs, present_v, log_prec, dyn, prior_var, obs_map, init,
    out, new_prec, loglik,
    words, table, nodes, vecs, ents, heads, head_vecs, power_rows, power_cols, lap_rhs, pair_rhs, step_rhs, drive, mask, offs, prior, filt,
    suffix, chunk8, in_buf, out_buf, off_buf, off_in, sum_buf, sum_in,
    chain_sem, off_send, off_recv, sum_send, sum_recv,
):
    pos = lax.axis_index("tm")
    states = dyn.shape[0]
    chunks = steps // WORD
    total = seqs * chunks
    levels = int(math.log2(chunks))
    first = [0]
    for level in range(1, levels + 1):
        first.append(first[-1] + (total >> (level - 1) if level > 1 else 0))

    in_buf[...] = jnp.zeros_like(in_buf)
    off_in[...] = jnp.zeros_like(off_in)
    barrier = pltpu.get_barrier_semaphore()
    for d in range(1, n):
        pl.semaphore_signal(barrier, inc=1, device_id={"tm": lax.rem(pos + d, n)}, device_id_type=MESH)

    lane = lax.broadcasted_iota(jnp.int32, (1, states), 1)
    active = (lane < sensors_s[0]).astype(F32)
    weight = jnp.exp(log_prec[...])
    weight_on = weight * active
    pv = prior_var[...]
    d_mat = dyn[...]
    d_t = d_mat.T
    h_mat = obs_map[...]
    h_rhs = stacked(h_mat)
    d_rhs = stacked(d_mat)
    readout = times(h_mat, d_rhs).T
    f_t = d_t - times(readout * weight_on, h_rhs) * pv

    for b in range(seqs):
        def word(k, b=b):
            t = k * WORD
            w = present_s[b, t]
            for i in range(1, WORD):
                w = w * 2 + present_s[b, t + i]
            words[b * chunks + k] = w
        over(chunks, 16, word)
        row = jnp.broadcast_to(present_v[b : b + 1, :].astype(F32), (steps, steps))
        same = lax.broadcasted_iota(jnp.int32, (steps, steps), 0) == lax.broadcasted_iota(jnp.int32, (steps, steps), 1)
        column = jnp.sum(jnp.where(same, row, 0.0), axis=1, keepdims=True)
        mask[b * steps : (b + 1) * steps, :] = jnp.broadcast_to(column, (steps, states))

    drive[...] = times(obs[...] * weight_on, h_rhs) * pv * mask[...]

    both = jnp.concatenate([d_t, f_t], axis=1)
    step_rhs[...] = stacked(both)
    pairs = []
    for a in (d_t, f_t):
        pairs.append(times(a, step_rhs[...]))
    pair_rhs[...] = stacked(jnp.concatenate(pairs, axis=1))
    for a in range(4):
        rows = pairs[a // 2][:, (a % 2) * states : (a % 2 + 1) * states]
        quad = times(rows, pair_rhs[...])
        for c in range(4):
            table[a * 4 + c] = stacked(quad[:, c * states : (c + 1) * states])

    def at(ref, i):
        return ref[pl.ds(i, total, stride=WORD), :]

    def advance(x, i):
        y = times(x, step_rhs[...])
        return jnp.where(at(mask, i) > 0.5, y[:, states:], y[:, :states]) + at(drive, i)

    x = at(drive, 0)
    for i in range(1, WORD):
        x = advance(x, i)
    offs[...] = x

    eye = (
        lax.broadcasted_iota(jnp.int32, (states, states), 0)
        == lax.broadcasted_iota(jnp.int32, (states, states), 1)
    ).astype(F32)
    residual = eye - times(d_t, d_rhs)
    by_one = times(jnp.concatenate([residual, d_mat], axis=0), d_rhs)
    r_1, d_2 = by_one[:states], by_one[states:]
    by_two = times(jnp.concatenate([residual, r_1, d_mat, d_2], axis=0), stacked(d_2))
    r_2, r_3 = by_two[:states], by_two[states : 2 * states]
    d_3, d_4 = by_two[2 * states : 3 * states], by_two[3 * states :]
    tail_rhs = stacked(jnp.concatenate([residual, r_1, r_2, r_3], axis=1))
    fill_rhs = stacked(jnp.concatenate([d_4, d_3, d_2, d_mat], axis=1))

    def keep_power(e, stack):
        if e < chunks:
            power_rows[e * 2 * states : (e + 1) * 2 * states, :] = stack
            power_cols[:, (chunks - 1 - e) * states : (chunks - e) * states] = stack
        else:
            lap_rhs[0 : 2 * states, :] = stack

    def power_of(e):
        return power_rows[e * 2 * states : (e + 1) * 2 * states, :]

    keep_power(0, stacked(eye))
    keep_power(1, stacked(d_4))

    for level in range(1, levels + 1):
        base, below = first[level], first[level - 1]

        def compose(j, level=level, base=base, below=below):
            if level == 1:
                left, right = table[words[2 * j]], table[words[2 * j + 1]]
                v_left, v_right = offs[pl.ds(2 * j, 1), :], offs[pl.ds(2 * j + 1, 1), :]
            else:
                left, right = nodes[below + 2 * j], nodes[below + 2 * j + 1]
                v_left, v_right = vecs[pl.ds(below + 2 * j, 1), :], vecs[pl.ds(below + 2 * j + 1, 1), :]
            rows = jnp.concatenate([left, stacked(jnp.broadcast_to(v_left, (8, states)))], axis=0)
            y = jnp.dot(twice(rows), right, preferred_element_type=F32)
            nodes[base + j] = stacked(y[:states] + y[states : 2 * states])
            vecs[pl.ds(base + j, 1), :] = (
                y[2 * states : 2 * states + 1] + y[2 * states + 8 : 2 * states + 9] + v_right
            )

        over(total >> level, total, compose)
        half = power_of(1 << (level - 1))
        keep_power(1 << level, stacked(product(twice(half), half)))

    def prepare():
        for b in range(seqs):
            rows = slice(b * 2 * states, (b + 1) * 2 * states)
            heads[rows, 0:states] = stacked(eye)
            for level in range(levels, 0, -1):
                for p in range(chunks >> level):
                    j = b * (chunks >> (level - 1)) + 2 * p
                    k = (p << level) + (1 << (level - 1))
                    if level == 1:
                        mat, v = table[words[j]], offs[j : j + 1, :]
                    else:
                        j = first[level - 1] + j
                        mat, v = nodes[j], vecs[j : j + 1, :]
                    if p > 0:
                        before = p << level
                        e_rows = head_vecs[b * chunks + before : b * chunks + before + 1, :]
                        left = jnp.concatenate(
                            [heads[rows, before * states : (before + 1) * states],
                             stacked(jnp.broadcast_to(e_rows, (8, states)))], axis=0)
                        y = jnp.dot(twice(left), mat, preferred_element_type=F32)
                        mat = stacked(y[:states] + y[states : 2 * states])
                        v = y[2 * states : 2 * states + 1] + y[2 * states + 8 : 2 * states + 9] + v
                    heads[rows, k * states : (k + 1) * states] = mat
                    head_vecs[b * chunks + k : b * chunks + k + 1, :] = v
        for level in range(1, levels):
            base = power_of(1 << level)
            for e in range(1, 1 << level):
                keep_power((1 << level) + e, stacked(product(twice(power_of(e)), base)))
        for d in range(1, n - 2):
            half = (d + 1) // 2 - 1
            other = d - 1 - half
            lap_rhs[d * 2 * states : (d + 1) * 2 * states, :] = stacked(
                product(
                    twice(lap_rhs[half * 2 * states : (half + 1) * 2 * states, :]),
                    lap_rhs[other * 2 * states : (other + 1) * 2 * states, :],
                )
            )

    head_vecs[...] = jnp.zeros_like(head_vecs)
    early = n // 2

    @pl.when(pos >= early)
    def _():
        prepare()

    pl.semaphore_wait(barrier, n - 1)
    row8 = lax.broadcasted_iota(jnp.int32, (8, states), 0)

    chain = pltpu.make_async_remote_copy(
        src_ref=out_buf, dst_ref=in_buf, send_sem=chain_sem.at[0], recv_sem=chain_sem.at[1],
        device_id={"tm": lax.rem(pos + 1, n)}, device_id_type=MESH,
    )

    @pl.when(pos == 0)
    def _():
        in_buf[0:seqs, :] = init[...]

    @pl.when(pos > 0)
    def _():
        chain.wait_recv()

    entering = in_buf[...]
    top = first[levels]
    left = jnp.concatenate(
        [twice(stacked(jnp.where(row8 == b, entering, 0.0))) for b in range(seqs)], axis=1
    )

    @pl.when(pos < n - 1)
    def _():
        leaving = product(left, nodes[top : top + seqs].reshape(seqs * 2 * states, states))
        for b in range(seqs):
            leaving = leaving + jnp.where(row8 == b, vecs[top + b : top + b + 1, :], 0.0)
        out_buf[...] = leaving
        chain.start()

    @pl.when(pos < early)
    def _():
        prepare()

    y = product(left, heads[...])
    for k in range(chunks):
        ents[pl.ds(k, seqs, stride=chunks), :] = y[0:seqs, k * states : (k + 1) * states]
    x = ents[...] + head_vecs[...]
    for i in range(WORD):
        prior[i * total : (i + 1) * total, :] = x
        x = advance(x, i)
        filt[i * total : (i + 1) * total, :] = x

    y = times(filt[...], tail_rhs)

    def part(i, k):
        return y[i * total : (i + 1) * total, k * states : (k + 1) * states]

    chunk8[...] = jnp.zeros_like(chunk8)
    for i in range(WORD):
        z = part(i, 0)
        for j in range(i + 1, WORD):
            z = z + part(j, j - i)
        suffix[i * total : (i + 1) * total, :] = z
        if i == 0:
            for b in range(seqs):
                chunk8[pl.ds(b, chunks, stride=8), :] = z[b * chunks : (b + 1) * chunks]

    last = jnp.zeros((8, states), F32)
    for b in range(seqs):
        r = (WORD - 1) * total + (b + 1) * chunks - 1
        last = jnp.where(row8 == b, jnp.broadcast_to(filt[r : r + 1, :], (8, states)), last)
    final = times(last, stacked(d_t))
    ends = chunk8[...].reshape(chunks, 8, states)
    left = jnp.concatenate([twice(stacked(ends[k])) for k in range(chunks)], axis=1)
    own = product(left, power_rows[...])
    own = own + jnp.where(pos == n - 1, times(final, lap_rhs[0 : 2 * states, :]), 0.0)
    off_buf[...] = own

    def send_off(d):
        return pltpu.make_async_remote_copy(
            src_ref=off_buf, dst_ref=off_in.at[d], send_sem=off_send.at[d], recv_sem=off_recv.at[d],
            device_id={"tm": lax.rem(pos + n - 1 - d, n)}, device_id_type=MESH,
        )

    for d in range(n - 1):
        @pl.when(pos - 1 - d >= 0)
        def _(d=d):
            send_off(d).start()

    obs_rows = [at(obs, i) for i in range(WORD)]
    mask_rows = [at(mask, i) for i in range(WORD)]
    errors = jnp.concatenate(obs_rows, axis=0) - times(prior[...], stacked(readout))
    seen = jnp.concatenate(mask_rows, axis=0)
    squares = jnp.sum(seen * active * errors * errors, axis=0, keepdims=True)
    number = jnp.sum(seen, axis=0, keepdims=True)
    sums = jnp.where(row8 == 0, jnp.broadcast_to(squares, (8, states)), jnp.broadcast_to(number, (8, states)))
    sum_buf[...] = sums

    def send_sum(d):
        return pltpu.make_async_remote_copy(
            src_ref=sum_buf, dst_ref=sum_in.at[d], send_sem=sum_send.at[d], recv_sem=sum_recv.at[d],
            device_id={"tm": lax.rem(pos + d + 1, n)}, device_id_type=MESH,
        )

    for d in range(n - 1):
        send_sum(d).start()

    ups = [ends]
    for level in range(levels):
        pair = ups[-1].reshape(ups[-1].shape[0] // 2, 2, 8, states)
        half = pair.shape[0]
        later = times(pair[:, 1].reshape(half * 8, states), power_of(1 << level))
        ups.append(pair[:, 0] + later.reshape(half, 8, states))
    x = jnp.zeros((1, 8, states), F32)
    for level in range(levels - 1, -1, -1):
        count = x.shape[0]
        pair = ups[level].reshape(count, 2, 8, states)
        if level == levels - 1:
            sooner = pair[:, 1]
        else:
            moved = times(x.reshape(count * 8, states), power_of(1 << level))
            sooner = moved.reshape(count, 8, states) + pair[:, 1]
        x = jnp.stack([sooner, x], axis=1).reshape(2 * count, 8, states)
    chunk8[...] = x.reshape(chunks * 8, states)

    for d in range(n - 1):
        @pl.when(pos + 1 + d < n)
        def _(d=d):
            send_off(d).wait_recv()

    left = jnp.concatenate([twice(stacked(off_in[d])) for d in range(1, n - 1)], axis=1)
    x = jnp.where(pos == n - 1, final, off_in[0] + product(left, lap_rhs[...]))
    y = times(x, power_cols[...])
    for k in range(chunks):
        chunk8[k * 8 : (k + 1) * 8, :] += y[:, k * states : (k + 1) * states]
    x = jnp.concatenate([chunk8[pl.ds(b, chunks, stride=8), :] for b in range(seqs)], axis=0)
    y = times(x, fill_rhs)
    for i in range(WORD):
        out[pl.ds(i, total, stride=WORD), :] = (
            suffix[i * total : (i + 1) * total, :] + y[:, i * states : (i + 1) * states]
        )

    for d in range(n - 1):
        send_sum(d).wait_recv()
        sums = sums + sum_in[d]
    squares, number = sums[0:1], sums[1:2]
    grad = 0.5 * active * (number - weight * squares)
    new_prec[...] = log_prec[...] + grad / (seqs * steps * n)
    terms = 0.5 * active * (log_prec[...] * number - weight * squares)
    loglik[...] = jnp.sum(terms, axis=1, keepdims=True) / (seqs * steps * n * states)

    @pl.when(pos < n - 1)
    def _():
        chain.wait_send()

    for d in range(n - 1):
        @pl.when(pos - 1 - d >= 0)
        def _(d=d):
            send_off(d).wait_send()
        send_sum(d).wait_send()


def local(n, obs, present, sensors, log_prec, dynamics, prior_var, obs_map, init_state):
    seqs, steps, channels = obs.shape
    states = dynamics.shape[0]
    chunks = steps // WORD
    total = seqs * chunks
    inner = sum(total >> level for level in range(1, int(math.log2(chunks)) + 1))
    vmem = pl.BlockSpec(memory_space=pltpu.VMEM)
    smem = pl.BlockSpec(memory_space=pltpu.SMEM)
    rows = seqs * steps
    smoothed, new_prec, loglik = pl.pallas_call(
        functools.partial(kernel, n, seqs, steps),
        out_shape=(
            jax.ShapeDtypeStruct((rows, states), F32),
            jax.ShapeDtypeStruct((1, channels), F32),
            jax.ShapeDtypeStruct((1, 1), F32),
        ),
        in_specs=[smem, smem] + [vmem] * 7,
        out_specs=(vmem, vmem, vmem),
        scratch_shapes=[
            pltpu.SMEM((total,), jnp.int32),
            pltpu.VMEM((2**WORD, 2 * states, states), BF16),
            pltpu.VMEM((inner, 2 * states, states), BF16),
            pltpu.VMEM(((inner + 7) // 8 * 8, states), F32),
            pltpu.VMEM((total, states), F32),
            pltpu.VMEM((seqs * 2 * states, chunks * states), BF16),
            pltpu.VMEM((total, states), F32),
            pltpu.VMEM((chunks * 2 * states, states), BF16),
            pltpu.VMEM((2 * states, chunks * states), BF16),
            pltpu.VMEM(((n - 2) * 2 * states, states), BF16),
            pltpu.VMEM((2 * states, 4 * states), BF16),
            pltpu.VMEM((2 * states, 2 * states), BF16),
            pltpu.VMEM((rows, states), F32),
            pltpu.VMEM((rows, states), F32),
            pltpu.VMEM((total, states), F32),
            pltpu.VMEM((rows, states), F32),
            pltpu.VMEM((rows, states), F32),
            pltpu.VMEM((rows, states), F32),
            pltpu.VMEM((chunks * 8, states), F32),
            pltpu.VMEM((8, states), F32),
            pltpu.VMEM((8, states), F32),
            pltpu.VMEM((8, states), F32),
            pltpu.VMEM((n, 8, states), F32),
            pltpu.VMEM((8, states), F32),
            pltpu.VMEM((n, 8, states), F32),
            pltpu.SemaphoreType.DMA((2,)),
            pltpu.SemaphoreType.DMA((n,)),
            pltpu.SemaphoreType.DMA((n,)),
            pltpu.SemaphoreType.DMA((n,)),
            pltpu.SemaphoreType.DMA((n,)),
        ],
        compiler_params=pltpu.CompilerParams(collective_id=0, has_side_effects=True),
        name="kalman",
    )(
        present, sensors, obs.reshape(rows, channels), present, log_prec.reshape(1, channels),
        dynamics, prior_var.reshape(1, states), obs_map, init_state,
    )
    return smoothed.reshape(seqs, steps, states), new_prec.reshape(channels), loglik.reshape(1)


def solution(mesh):
    in_specs = (
        P("cluster", "tm", None),
        P("cluster", "tm"),
        P("cluster"),
        P("cluster"),
        P("cluster", None),
        P("cluster"),
        P("cluster", None),
        P("cluster", None),
    )
    out_specs = (P("cluster", "tm", None), P("cluster"), P("cluster"))
    body = functools.partial(local, mesh.shape["tm"])
    return jax.shard_map(body, mesh=mesh, in_specs=in_specs, out_specs=out_specs, check_vma=False)
```

profile of v0, /device:TPU:0, one launch (start us, length us, event | category | flops | bytes accessed | tf_op | source)
XLA Modules:
  0.0 27.7 jit_solution(7914782801478040894)
XLA Ops:
  1.3 22.5 %kalman.1 = (f32[192,128]{1,0:T(8,128)}, f32[1,128]{1,0:T(1,128)}, f32[1,1]{1,0:T(1,128)}) custom-call(s32[3,64]{1,0:T(4,128)} %present_v.1, s32[1]{0:T(128)S(6)} %copy.14.sensors_s, f32[192,128]{1,0:T(8,128)} %bitcast.7, s32[3,64]{1,0:T(4,128)} %present_v.1, f32[1,128]{1,0:T(1,128)} %bitcast.8, f32[128,128]{1,0:T(8,128)} %dyn.1, f32[1,128]{1,0:T(1,128)} %bitcast.9, ...), custom_call_target="tpu_custom_call" | custom-call | tf_op jit(solution)/shard_map/kalman/pallas_call | solution.py:380
  23.8 0.0 copy-start
  23.8 1.5 %copy.15 = f32[3,64,128]{2,1,0:T(8,128)} copy(f32[3,64,128]{2,1,0:T(8,128)} %bitcast.6) | data formatting | bytes 196608
  25.3 0.0 copy-done
  25.4 0.5 %copy.16 = f32[128]{0:T(128)} copy(f32[128]{0:T(128)S(1)} %bitcast.10) | data formatting | bytes 1024
Async XLA Ops:
  23.8 1.6 %copy-start = (f32[1,128]{1,0:T(1,128)S(1)}, f32[1,128]{1,0:T(1,128)}, u32[]{:S(2)}) copy-start(f32[1,128]{1,0:T(1,128)} %get-tuple-element.7) | copy-start | bytes 1540
where the time goes:
time: 27.9 us; the launch traced here: 27.7 us
  Pallas kernels  22.5 us (81%)
  between operations  3.11 us (11%)
  local copies, waits for them, and re-layouts  2.06 us (7%)
    pallas_call x1, Pallas kernels, local(): pl.pallas_call(functools.partial(kernel, n, seqs, steps), out_shape=(jax....  22.5 us
    unnamed x4, local copies, waits for them, and re-layouts  2.06 us

commit v1 on v0

--- a/solution.py
+++ b/solution.py
@@ -355,7 +355,7 @@
     grad = 0.5 * active * (number - weight * squares)
     new_prec[...] = log_prec[...] + grad / (seqs * steps * n)
     terms = 0.5 * active * (log_prec[...] * number - weight * squares)
-    loglik[...] = jnp.sum(terms, axis=1, keepdims=True) / (seqs * steps * n * states)
+    loglik[...] = jnp.zeros_like(terms) + jnp.sum(terms, axis=1, keepdims=True) / (seqs * steps * n * states)
 
     @pl.when(pos < n - 1)
     def _():
@@ -366,6 +366,12 @@
         def _(d=d):
             send_off(d).wait_send()
         send_sum(d).wait_send()
+
+
+def finish(smoothed, new_prec, loglik, out, out_prec, out_loglik):
+    out[...] = smoothed[...]
+    out_prec[...] = new_prec[...]
+    out_loglik[...] = loglik[:, 0:1]
 
 
 def local(n, obs, present, sensors, log_prec, dynamics, prior_var, obs_map, init_state):
@@ -380,9 +386,9 @@
     smoothed, new_prec, loglik = pl.pallas_call(
         functools.partial(kernel, n, seqs, steps),
         out_shape=(
-            jax.ShapeDtypeStruct((rows, states), F32),
-            jax.ShapeDtypeStruct((1, channels), F32),
-            jax.ShapeDtypeStruct((1, 1), F32),
+            pltpu.VMEM((rows, states), F32),
+            pltpu.VMEM((1, channels), F32),
+            pltpu.VMEM((1, channels), F32),
         ),
         in_specs=[smem, smem] + [vmem] * 7,
         out_specs=(vmem, vmem, vmem),
@@ -424,6 +430,18 @@
         present, sensors, obs.reshape(rows, channels), present, log_prec.reshape(1, channels),
         dynamics, prior_var.reshape(1, states), obs_map, init_state,
     )
+    held = [pltpu.with_memory_space_constraint(a, pltpu.VMEM) for a in (smoothed, new_prec, loglik)]
+    smoothed, new_prec, loglik = pl.pallas_call(
+        finish,
+        out_shape=(
+            jax.ShapeDtypeStruct((rows, states), F32),
+            jax.ShapeDtypeStruct((1, channels), F32),
+            jax.ShapeDtypeStruct((1, 1), F32),
+        ),
+        in_specs=[vmem] * 3,
+        out_specs=(vmem, vmem, vmem),
+        name="finish",
+    )(*held)
     return smoothed.reshape(seqs, steps, states), new_prec.reshape(channels), loglik.reshape(1)
 
 

time: 27.9 us -> 24 us (0.86)
  local copies, waits for them, and re-layouts: 2.06 us -> 0 us
  between operations: 3.11 us -> 1.29 us
    unnamed x4 -> x0, local copies, waits for them, and re-layouts: 2.06 us -> none
    pallas_call x1 -> x2, Pallas kernels: 22.5 us -> 22.5 us  [the longest x1 21.9 us: local(): pl.pallas_call(functools.partial(kernel, n, seqs, steps), out_shape=(pltp...]
where the time goes in v1:
time: 24 us; the launch traced here: 23.8 us
  Pallas kernels  22.5 us (94%)
  between operations  1.29 us (5%)
    pallas_call x1, Pallas kernels, local(): pl.pallas_call(functools.partial(kernel, n, seqs, steps), out_shape=(pltp...  21.9 us
    pallas_call x1, Pallas kernels, local(): pl.pallas_call(finish, out_shape=(jax.ShapeDtypeStruct((rows, states), F3...  0.65 us

profile of v1, /device:TPU:0, one launch (start us, length us, event | category | flops | bytes accessed | tf_op | source)
XLA Modules:
  0.0 23.8 jit_solution(320298508497797503)
XLA Ops:
  1.3 21.9 %kalman.1 = (f32[192,128]{1,0:T(8,128)S(1)}, f32[1,128]{1,0:T(1,128)S(1)}, f32[1,128]{1,0:T(1,128)S(1)}) custom-call(s32[3,64]{1,0:T(4,128)} %present_v.1, s32[1]{0:T(128)S(6)} %copy.11.sensors_s, f32[192,128]{1,0:T(8,128)} %bitcast.6, s32[3,64]{1,0:T(4,128)} %present_v.1, f32[1,128]{1,0:T(1,128)} %bitcast.7, f32[128,128]{1,0:T(8,128)} %dyn.1, ...), custom_call_target="tpu_custom_call" | custom-call | tf_op jit(solution)/shard_map/kalman/pallas_call | solution.py:386
  23.2 0.7 %finish.1 = (f32[192,128]{1,0:T(8,128)}, f32[1,128]{1,0:T(1,128)}, f32[1,1]{1,0:T(1,128)}) custom-call(f32[192,128]{1,0:T(8,128)S(1)} %get-tuple-element.9.smoothed, f32[1,128]{1,0:T(1,128)S(1)} %get-tuple-element.10.new_prec, f32[1,128]{1,0:T(1,128)S(1)} %get-tuple-element.11.loglik), custom_call_target="tpu_custom_call" | custom-call | tf_op jit(solution)/shard_map/finish/pallas_call | solution.py:434

commit v2 on v1

v2 whole, which is shorter than its diff:
```python
import functools
import math

import jax
import jax.numpy as jnp
from jax import lax
from jax.experimental import pallas as pl
from jax.experimental.pallas import tpu as pltpu
from jax.sharding import PartitionSpec as P

F32 = jnp.float32
BF16 = jnp.bfloat16
MESH = pl.DeviceIdType.MESH
WORD = 4
EXTRA = 8


def split(a):
    high = a.astype(BF16).astype(F32)
    return jnp.concatenate([high, a - high], axis=1).astype(BF16)


def stacked(a):
    high = a.astype(BF16).astype(F32)
    return jnp.concatenate([high, a - high], axis=0).astype(BF16)


def deep(node):
    return jnp.concatenate([node, node], axis=0)


def tall(node):
    width = node.shape[1] // 2
    return jnp.concatenate([node[:, :width], node[:, width:]], axis=0)


def twice(s):
    return jnp.concatenate([s, s], axis=1)


def product(left, right):
    full = jnp.dot(left, right, preferred_element_type=F32)
    rows = full.shape[0] // 2
    return full[:rows] + full[rows:]


def times(a, right):
    return product(twice(stacked(a)), right)


def wide(left, right):
    full = jnp.dot(left, right, preferred_element_type=F32)
    half = left.shape[1] // 2 if left.shape[1] < 256 else 128
    return [
        full[:, 2 * k * half : (2 * k + 1) * half] + full[:, (2 * k + 1) * half : (2 * k + 2) * half]
        for k in range(full.shape[1] // (2 * half))
    ]


def mul(a, node):
    return wide(split(a), deep(node))[0]


def kernel(
    n, seqs, steps,
    present_s, sensors_s, obs, present_v, log_prec, dyn, prior_var, obs_map, init,
    out, new_prec, loglik,
    words, table, theta, theta_4, nodes, vecs, psi_f, psi_n, us, offs, u_rows, u_4, ents, powers, laps, step_rhs,
    drive, mask, prior, filt, suffix, chunk8,
    even_node, even_v, pair_node, pair_v, prev_node, prev_v, omega_node, omega_v, psi_own, psi_v, state,
    vec_in, vec_out, vec_back, mat_out, mat_in, comp_out, comp_in, psi_out, psi_in,
    off_out, off_in, near_out, near_in, sum_buf, sum_in,
    vec_send, vec_recv, mat_sem, comp_sem, psi_sem, near_sem, off_send, off_recv, sum_send, sum_recv,
):
    pos = lax.axis_index("tm")
    par = lax.rem(pos, 2)
    quarter = lax.rem(pos, 4)
    chip = lax.div(pos, 2)
    chips = n // 2
    states = dyn.shape[0]
    block = states + EXTRA
    chunks = steps // WORD
    total = seqs * chunks
    levels = int(math.log2(chunks))
    first = [0]
    for level in range(1, levels + 1):
        first.append(first[-1] + (total >> (level - 1) if level > 1 else 0))
    top = first[levels]

    vec_in[...] = jnp.zeros_like(vec_in)
    off_in[...] = jnp.zeros_like(off_in)
    near_in[...] = jnp.zeros_like(near_in)
    barrier = pltpu.get_barrier_semaphore()
    for d in range(1, n):
        pl.semaphore_signal(barrier, inc=1, device_id={"tm": lax.rem(pos + d, n)}, device_id_type=MESH)

    lane = lax.broadcasted_iota(jnp.int32, (1, states), 1)
    row8 = lax.broadcasted_iota(jnp.int32, (8, states), 0)
    active = (lane < sensors_s[0]).astype(F32)
    weight = jnp.exp(log_prec[...])
    weight_on = weight * active
    pv = prior_var[...]
    d_mat = dyn[...]
    d_t = d_mat.T
    h_mat = obs_map[...]
    h_2 = split(h_mat)
    d_2n = split(d_mat)
    d_t2 = split(d_t)
    readout = wide(d_t2, deep(split(h_mat.T)))[0]
    f_t = d_t - mul(readout * weight_on, h_2) * pv
    f_t2 = split(f_t)

    for b in range(seqs):
        for k in range(chunks):
            t = k * WORD
            w = present_s[b, t]
            for i in range(1, WORD):
                w = w * 2 + present_s[b, t + i]
            words[b * chunks + k] = w
        row = jnp.broadcast_to(present_v[b : b + 1, :].astype(F32), (steps, steps))
        same = lax.broadcasted_iota(jnp.int32, (steps, steps), 0) == lax.broadcasted_iota(jnp.int32, (steps, steps), 1)
        column = jnp.sum(jnp.where(same, row, 0.0), axis=1, keepdims=True)
        mask[b * steps : (b + 1) * steps, :] = jnp.broadcast_to(column, (steps, states))

    drive[...] = mul(obs[...] * weight_on, h_2) * pv * mask[...]

    step_rhs[...] = stacked(jnp.concatenate([d_t, f_t], axis=1))
    singles = [d_t2, f_t2]
    both = deep(jnp.concatenate(singles, axis=1))
    pairs = []
    for a in range(2):
        pairs += [split(q) for q in wide(singles[a], both)]
    quad_rhs = deep(jnp.concatenate(pairs, axis=1))
    for a in range(4):
        quad = wide(pairs[a], quad_rhs)
        for c in range(4):
            table[a * 4 + c] = split(quad[c])

    def at(ref, i):
        return ref[pl.ds(i, total, stride=WORD), :]

    def advance(x, i):
        y = times(x, step_rhs[...])
        return jnp.where(at(mask, i) > 0.5, y[:, states:], y[:, :states]) + at(drive, i)

    zero_states = [at(drive, 0)]
    for i in range(1, WORD):
        zero_states.append(advance(zero_states[-1], i))
    offs[...] = zero_states[-1]

    def leading(matrix, v):
        return jnp.concatenate([matrix, split(jnp.broadcast_to(v, (16, states)))], axis=0)

    def child(level, j):
        if level == 1:
            return table[words[j]], offs[j : j + 1, :]
        j = first[level - 1] + j
        return nodes[j], vecs[j : j + 1, :]

    for level in range(1, levels + 1):
        for j in range(total >> level):
            left, v_left = child(level, 2 * j)
            right, v_right = child(level, 2 * j + 1)
            y = wide(leading(left, v_left), deep(right))[0]
            j = first[level] + j
            v = y[states : states + EXTRA] + v_right
            nodes[j] = split(y[:states])
            vecs[j : j + 1, :] = v[0:1]
            if level == levels:
                b = j - top
                mat_out[b * block : b * block + states, :] = y[:states]
                mat_out[b * block + states : (b + 1) * block, :] = v

    def lefts(x):
        return jnp.concatenate([twice(stacked(jnp.where(row8 == b, x, 0.0))) for b in range(seqs)], axis=1)

    def apply(left, node, v):
        rhs = jnp.concatenate([tall(node[b]) for b in range(seqs)], axis=0)
        return product(left, rhs) + v

    def rows_of(ref):
        v = jnp.zeros((8, states), F32)
        for b in range(seqs):
            v = jnp.where(row8 == b, ref[b * block + states : (b + 1) * block, :], v)
        return v

    own = nodes.at[pl.ds(top, seqs)]

    def own_v():
        v = jnp.zeros((8, states), F32)
        for b in range(seqs):
            v = jnp.where(row8 == b, vecs[top + b : top + b + 1, :], v)
        return v

    def send_vec(src, slot, to):
        return pltpu.make_async_remote_copy(
            src_ref=src, dst_ref=vec_in, send_sem=vec_send.at[slot], recv_sem=vec_recv,
            device_id={"tm": to}, device_id_type=MESH,
        )

    def shift(by):
        return lax.rem(pos + (by + n), n)

    def send_mat(src, dst, sem, by):
        return pltpu.make_async_remote_copy(
            src_ref=src, dst_ref=dst, send_sem=sem.at[0], recv_sem=sem.at[1],
            device_id={"tm": shift(by)}, device_id_type=MESH,
        )

    mat = send_mat(mat_out, mat_in, mat_sem, 1)
    comp = send_mat(comp_out, comp_in, comp_sem, 2)
    psi = send_mat(psi_out, psi_in, psi_sem, 1)
    near = send_mat(near_out, near_in, near_sem, -1)
    to_next = [send_vec(vec_out, k, shift(by)) for k, by in enumerate((1, 2, 4))]
    to_back = send_vec(vec_back, 3, shift(-1))

    even = par == 0
    odd = par == 1
    has_mat = jnp.logical_and(odd, pos >= 2)
    gives_mat = jnp.logical_and(even, pos >= 2)
    gives_comp = jnp.logical_and(quarter == 1, pos >= 4)
    has_comp = jnp.logical_and(quarter == 3, pos >= 4)
    last_of_four = jnp.logical_and(quarter == 3, pos < n - 1)

    pl.semaphore_wait(barrier, n - 1)

    @pl.when(gives_mat)
    def _():
        mat.start()

    @pl.when(pos == 0)
    def _():
        vec_in[0:seqs, :] = init[...]
        vec_out[...] = apply(lefts(vec_in[...]), own, own_v())
        to_next[0].start()

    eye = (
        lax.broadcasted_iota(jnp.int32, (states, states), 0)
        == lax.broadcasted_iota(jnp.int32, (states, states), 1)
    ).astype(F32)
    residual = eye - mul(d_t, d_2n)
    r_1, d_2 = [mul(a, d_2n) for a in (residual, d_mat)]
    d_2s = split(d_2)
    r_2, r_3, d_3, d_4 = [mul(a, d_2s) for a in (residual, r_1, d_mat, d_2)]
    d_4s = split(d_4)
    tails = [split(a) for a in (residual, r_1, r_2, r_3)]
    powers[0] = split(eye)
    powers[1] = d_4s
    left = jnp.concatenate([twice(stacked(z)) for z in zero_states], axis=1)
    u = product(left, jnp.concatenate([tall(a) for a in tails], axis=0))
    u_rows[...] = u
    u_4[...] = times(u, tall(d_4s))
    theta_2 = []
    for a in range(4):
        left = jnp.concatenate([singles[a // 2], pairs[a]], axis=1)
        rhs = jnp.concatenate([deep(tails[0]), deep(tails[1])], axis=0)
        theta_2.append(wide(left, rhs)[0])
    theta_rhs = deep(jnp.concatenate([split(mul(a, d_2s)) for a in theta_2], axis=1))
    for a in range(4):
        full = wide(pairs[a], theta_rhs)
        for c in range(4):
            whole = theta_2[a] + full[c]
            theta[a * 4 + c] = whole
            theta_4[a * 4 + c] = split(mul(whole, d_4s))

    @pl.when(pos == 1)
    def _():
        to_back.wait_recv()
        vec_out[...] = apply(lefts(vec_in[...]), own, own_v())
        to_next[0].start()
        to_next[1].start()

    @pl.when(has_mat)
    def _():
        mat.wait_recv()
        even_v[...] = rows_of(mat_in)
        for b in range(seqs):
            left = split(mat_in[b * block : b * block + states, :])
            even_node[b] = left
            v_left = mat_in[b * block + states : b * block + states + 1, :]
            y = wide(leading(left, v_left), deep(nodes[top + b]))[0]
            pair_node[b] = split(y[:states])
            comp_out[b * block : b * block + states, :] = y[:states]
            comp_out[b * block + states : (b + 1) * block, :] = y[states : states + EXTRA] + vecs[top + b : top + b + 1, :]
        pair_v[...] = rows_of(comp_out)

    @pl.when(gives_comp)
    def _():
        comp.start()

    @pl.when(pos == 3)
    def _():
        to_back.wait_recv()
        vec_out[...] = apply(lefts(vec_in[...]), pair_node, pair_v[...])

        @pl.when(pos < n - 1)
        def _():
            for copy in to_next:
                copy.start()

    for level in range(1, levels + 1):
        lag = powers[1 << (level - 1)]
        for j in range(total >> level):
            left, v_left = child(level, 2 * j)
            lead = leading(left, v_left)
            a, b = 2 * j, 2 * j + 1
            if level == 1:
                y = wide(lead, deep(theta_4[words[b]]))[0]
                whole = theta[words[a]] + y[:states]
                u = y[states : states + EXTRA] + u_4[b : b + 1, :] + u_rows[a : a + 1, :]
            else:
                a, b = first[level - 1] + a, first[level - 1] + b
                y = wide(lead, deep(psi_n[b]))[0]
                y = jnp.concatenate([y[:states], y[states:] + us[b : b + 1, :]], axis=0)
                y = mul(y, lag)
                whole = psi_f[a] + y[:states]
                u = y[states : states + EXTRA] + us[a : a + 1, :]
            k = first[level] + j
            if level == levels:
                psi_out[j * block : j * block + states, :] = whole
                psi_out[j * block + states : (j + 1) * block, :] = u
            else:
                us[k : k + 1, :] = u[0:1]
                if j % 2 == 0:
                    psi_f[k] = whole
                else:
                    psi_n[k] = split(whole)
        if level < levels:
            base = powers[1 << (level - 1)]
            for e in range(1, (1 << (level - 1)) + 1):
                made = mul_node(powers[e], base)
                powers[(1 << (level - 1)) + e] = made
    base = powers[chunks // 2]
    for e in range(1, chunks // 2 + 1):
        powers[chunks // 2 + e] = mul_node(powers[e], base)
    lap = powers[chunks]
    laps[0] = powers[0]
    laps[1] = lap
    for m in range(2, 2 * chips - 2):
        laps[m] = mul_node(laps[m // 2], laps[m - m // 2])

    @pl.when(gives_mat)
    def _():
        psi.start()

    @pl.when(pos == n - 1)
    def _():
        close = split(mul(d_t, lap))
        for b in range(seqs):
            y = wide(leading(nodes[top + b], vecs[top + b : top + b + 1, :]), deep(close))[0]
            psi_out[b * block : (b + 1) * block, :] += y[:block]

    for b in range(seqs):
        psi_own[b] = split(psi_out[b * block : b * block + states, :])
    psi_v[...] = rows_of(psi_out)

    @pl.when(has_mat)
    def _():
        parts = []
        for b in range(seqs):
            v_left = mat_in[b * block + states : b * block + states + 1, :]
            y = wide(leading(even_node[b], v_left), deep(psi_own[b]))[0]
            u = psi_out[b * block + states : b * block + states + 1, :]
            y = jnp.concatenate([y[:states], y[states:] + u], axis=0)
            parts.append(mul(y, lap)[:block])
        psi.wait_recv()
        for b in range(seqs):
            psi_in[b * block : (b + 1) * block, :] += parts[b]
            omega_node[b] = split(psi_in[b * block : b * block + states, :])
        omega_v[...] = rows_of(psi_in)

    def send_off(d, side):
        return pltpu.make_async_remote_copy(
            src_ref=off_out, dst_ref=off_in.at[d - 1], send_sem=off_send.at[2 * d - 2 + side], recv_sem=off_recv.at[d - 1],
            device_id={"tm": lax.rem(2 * (chip + chips - d) + side, n)}, device_id_type=MESH,
        )

    @pl.when(jnp.logical_or(pos == 2, pos >= 4))
    def _():
        to_back.wait_recv()

    @pl.when(has_comp)
    def _():
        comp.wait_recv()
        prev_v[...] = rows_of(comp_in)
        for b in range(seqs):
            prev_node[b] = split(comp_in[b * block : b * block + states, :])
        back = apply(lefts(vec_in[...]), prev_node, prev_v[...])
        vec_back[...] = back
        to_back.start()
        state[...] = back

    @pl.when(jnp.logical_not(has_comp))
    def _():
        state[...] = vec_in[...]

    @pl.when(jnp.logical_and(has_comp, pos < n - 1))
    def _():
        vec_out[...] = apply(lefts(state[...]), pair_node, pair_v[...])
        for copy in to_next:
            copy.start()

    @pl.when(has_mat)
    def _():
        left = lefts(state[...])
        off_out[...] = apply(left, omega_node, omega_v[...])
        for d in range(1, chips):
            @pl.when(chip - d >= 0)
            def _(d=d):
                send_off(d, 1).start()
                send_off(d, 0).start()
        state[...] = apply(left, even_node, even_v[...])

    @pl.when(odd)
    def _():
        near_out[...] = apply(lefts(state[...]), psi_own, psi_v[...])
        near.start()

    x = state[...]
    entering = []
    for b in range(seqs):
        entering.append(jnp.broadcast_to(x[b : b + 1], (8, states)))
    for level in range(levels, 0, -1):
        below = []
        for j in range(total >> level):
            node, v = child(level, 2 * j)
            below.append(entering[j])
            below.append(times(entering[j], tall(node)) + v)
        entering = below
    for j in range(total):
        ents[j : j + 1, :] = entering[j][0:1]

    x = ents[...]
    for i in range(WORD):
        prior[i * total : (i + 1) * total, :] = x
        x = advance(x, i)
        filt[i * total : (i + 1) * total, :] = x

    chunk8[...] = jnp.zeros_like(chunk8)
    for i in range(WORD):
        left = jnp.concatenate([twice(stacked(filt[j * total : (j + 1) * total, :])) for j in range(i, WORD)], axis=1)
        z = product(left, jnp.concatenate([tall(tails[j]) for j in range(WORD - i)], axis=0))
        suffix[i * total : (i + 1) * total, :] = z
        if i == 0:
            for b in range(seqs):
                chunk8[pl.ds(b, chunks, stride=8), :] = z[b * chunks : (b + 1) * chunks]
    ends = chunk8[...].reshape(chunks, 8, states)

    errors = jnp.concatenate([at(obs, i) for i in range(WORD)], axis=0) - mul(prior[...], split(readout))
    seen = jnp.concatenate([at(mask, i) for i in range(WORD)], axis=0)
    squares = jnp.sum(seen * active * errors * errors, axis=0, keepdims=True)
    number = jnp.sum(seen, axis=0, keepdims=True)
    sums = jnp.where(row8 == 0, jnp.broadcast_to(squares, (8, states)), jnp.broadcast_to(number, (8, states)))
    sum_buf[...] = sums

    def send_sum(d):
        return pltpu.make_async_remote_copy(
            src_ref=sum_buf, dst_ref=sum_in.at[d], send_sem=sum_send.at[d], recv_sem=sum_recv.at[d],
            device_id={"tm": lax.rem(pos + d + 1, n)}, device_id_type=MESH,
        )

    for d in range(n - 1):
        send_sum(d).start()

    last = jnp.zeros((8, states), F32)
    for b in range(seqs):
        r = (WORD - 1) * total + (b + 1) * chunks - 1
        last = jnp.where(row8 == b, jnp.broadcast_to(filt[r : r + 1, :], (8, states)), last)
    final = times(last, tall(d_t2))

    ups = [ends]
    for level in range(levels):
        pair = ups[-1].reshape(ups[-1].shape[0] // 2, 2, 8, states)
        half = pair.shape[0]
        later = times(pair[:, 1].reshape(half * 8, states), tall(powers[1 << level]))
        ups.append(pair[:, 0] + later.reshape(half, 8, states))
    x = jnp.zeros((1, 8, states), F32)
    for level in range(levels - 1, -1, -1):
        count = x.shape[0]
        pair = ups[level].reshape(count, 2, 8, states)
        if level == levels - 1:
            sooner = pair[:, 1]
        else:
            moved = times(x.reshape(count * 8, states), tall(powers[1 << level]))
            sooner = moved.reshape(count, 8, states) + pair[:, 1]
        x = jnp.stack([sooner, x], axis=1).reshape(2 * count, 8, states)
    chunk8[...] = x.reshape(chunks * 8, states)

    @pl.when(even)
    def _():
        near.wait_recv()

    for d in range(1, chips):
        @pl.when(chip + d < chips)
        def _(d=d):
            send_off(d, 0).wait_recv()

    left = jnp.concatenate([twice(stacked(off_in[d])) for d in range(chips - 1)], axis=1)
    rhs = jnp.concatenate([tall(laps[2 * d + 1 - par]) for d in range(chips - 1)], axis=0)
    x = jnp.where(pos == n - 1, final, near_in[...] + product(left, rhs))
    y = times(x, jnp.concatenate([tall(powers[chunks - 1 - k]) for k in range(chunks)], axis=1))
    for k in range(chunks):
        chunk8[k * 8 : (k + 1) * 8, :] += y[:, k * states : (k + 1) * states]
    x = jnp.concatenate([chunk8[pl.ds(b, chunks, stride=8), :] for b in range(seqs)], axis=0)
    y = times(x, jnp.concatenate([tall(a) for a in (d_4s, split(d_3), d_2s, d_2n)], axis=1))
    for i in range(WORD):
        out[pl.ds(i, total, stride=WORD), :] = (
            suffix[i * total : (i + 1) * total, :] + y[:, i * states : (i + 1) * states]
        )

    for d in range(n - 1):
        send_sum(d).wait_recv()
        sums = sums + sum_in[d]
    squares, number = sums[0:1], sums[1:2]
    grad = 0.5 * active * (number - weight * squares)
    new_prec[...] = log_prec[...] + grad / (seqs * steps * n)
    terms = 0.5 * active * (log_prec[...] * number - weight * squares)
    loglik[...] = jnp.zeros_like(terms) + jnp.sum(terms, axis=1, keepdims=True) / (seqs * steps * n * states)

    @pl.when(gives_mat)
    def _():
        mat.wait_send()
        psi.wait_send()

    @pl.when(gives_comp)
    def _():
        comp.wait_send()

    @pl.when(pos == 0)
    def _():
        to_next[0].wait_send()

    @pl.when(pos == 1)
    def _():
        to_next[0].wait_send()
        to_next[1].wait_send()

    @pl.when(last_of_four)
    def _():
        for copy in to_next:
            copy.wait_send()

    @pl.when(has_comp)
    def _():
        to_back.wait_send()

    @pl.when(odd)
    def _():
        near.wait_send()

    for d in range(1, chips):
        @pl.when(jnp.logical_and(has_mat, chip - d >= 0))
        def _(d=d):
            send_off(d, 0).wait_send()
            send_off(d, 1).wait_send()

    for d in range(n - 1):
        send_sum(d).wait_send()


def mul_node(left, right):
    return split(wide(left, deep(right))[0])


def finish(smoothed, new_prec, loglik, out, out_prec, out_loglik):
    out[...] = smoothed[...]
    out_prec[...] = new_prec[...]
    out_loglik[...] = loglik[:, 0:1]


def local(n, obs, present, sensors, log_prec, dynamics, prior_var, obs_map, init_state):
    seqs, steps, channels = obs.shape
    states = dynamics.shape[0]
    assert n % 4 == 0 and states == 128 and channels == 128
    chunks = steps // WORD
    total = seqs * chunks
    chips = n // 2
    inner = sum(total >> level for level in range(1, int(math.log2(chunks)) + 1))
    vmem = pl.BlockSpec(memory_space=pltpu.VMEM)
    smem = pl.BlockSpec(memory_space=pltpu.SMEM)
    rows = seqs * steps
    block = seqs * (states + EXTRA)
    node = (states, 2 * states)
    tile = pltpu.VMEM((8, states), F32)
    whole = pltpu.VMEM((block, states), F32)
    level_rows = (inner + 7) // 8 * 8
    dma = pltpu.SemaphoreType.DMA
    smoothed, new_prec, loglik = pl.pallas_call(
        functools.partial(kernel, n, seqs, steps),
        out_shape=(
            pltpu.VMEM((rows, states), F32),
            pltpu.VMEM((1, channels), F32),
            pltpu.VMEM((1, channels), F32),
        ),
        in_specs=[smem, smem] + [vmem] * 7,
        out_specs=(vmem, vmem, vmem),
        scratch_shapes=[
            pltpu.SMEM((total,), jnp.int32),
            pltpu.VMEM((2**WORD,) + node, BF16),
            pltpu.VMEM((2**WORD, states, states), F32),
            pltpu.VMEM((2**WORD,) + node, BF16),
            pltpu.VMEM((inner,) + node, BF16),
            pltpu.VMEM((level_rows, states), F32),
            pltpu.VMEM((inner, states, states), F32),
            pltpu.VMEM((inner,) + node, BF16),
            pltpu.VMEM((level_rows, states), F32),
            pltpu.VMEM((total, states), F32),
            pltpu.VMEM((total, states), F32),
            pltpu.VMEM((total, states), F32),
            pltpu.VMEM((total, states), F32),
            pltpu.VMEM((chunks + 1,) + node, BF16),
            pltpu.VMEM((2 * chips - 2,) + node, BF16),
            pltpu.VMEM((2 * states, 2 * states), BF16),
            pltpu.VMEM((rows, states), F32),
            pltpu.VMEM((rows, states), F32),
            pltpu.VMEM((rows, states), F32),
            pltpu.VMEM((rows, states), F32),
            pltpu.VMEM((rows, states), F32),
            pltpu.VMEM((chunks * 8, states), F32),
            pltpu.VMEM((seqs,) + node, BF16), tile,
            pltpu.VMEM((seqs,) + node, BF16), tile,
            pltpu.VMEM((seqs,) + node, BF16), tile,
            pltpu.VMEM((seqs,) + node, BF16), tile,
            pltpu.VMEM((seqs,) + node, BF16), tile,
            tile,
            tile, tile, tile, whole, whole, whole, whole, whole, whole,
            tile, pltpu.VMEM((chips - 1, 8, states), F32), tile, tile, tile, pltpu.VMEM((n, 8, states), F32),
            dma((4,)), dma(()), dma((2,)), dma((2,)), dma((2,)), dma((2,)),
            dma((2 * chips - 2,)), dma((chips - 1,)), dma((n,)), dma((n,)),
        ],
        compiler_params=pltpu.CompilerParams(collective_id=0, has_side_effects=True),
        name="kalman",
    )(
        present, sensors, obs.reshape(rows, channels), present, log_prec.reshape(1, channels),
        dynamics, prior_var.reshape(1, states), obs_map, init_state,
    )
    held = [pltpu.with_memory_space_constraint(a, pltpu.VMEM) for a in (smoothed, new_prec, loglik)]
    smoothed, new_prec, loglik = pl.pallas_call(
        finish,
        out_shape=(
            jax.ShapeDtypeStruct((rows, states), F32),
            jax.ShapeDtypeStruct((1, channels), F32),
            jax.ShapeDtypeStruct((1, 1), F32),
        ),
        in_specs=[vmem] * 3,
        out_specs=(vmem, vmem, vmem),
        name="finish",
    )(*held)
    return smoothed.reshape(seqs, steps, states), new_prec.reshape(channels), loglik.reshape(1)


def solution(mesh):
    in_specs = (
        P("cluster", "tm", None),
        P("cluster", "tm"),
        P("cluster"),
        P("cluster"),
        P("cluster", None),
        P("cluster"),
        P("cluster", None),
        P("cluster", None),
    )
    out_specs = (P("cluster", "tm", None), P("cluster"), P("cluster"))
    body = functools.partial(local, mesh.shape["tm"])
    return jax.shard_map(body, mesh=mesh, in_specs=in_specs, out_specs=out_specs, check_vma=False)
```

time: 24 us -> 19.8 us (0.83)
  Pallas kernels: 22.5 us -> 18.4 us
    pallas_call x1, Pallas kernels: 21.9 us -> 17.7 us  [local(): pl.pallas_call(functools.partial(kernel, n, seqs, steps), out_shape=(pltp...]
where the time goes in v2:
time: 19.8 us; the launch traced here: 19.7 us
  Pallas kernels  18.4 us (93%)
  between operations  1.29 us (7%)
    pallas_call x1, Pallas kernels, local(): pl.pallas_call(functools.partial(kernel, n, seqs, steps), out_shape=(pltp...  17.7 us
    pallas_call x1, Pallas kernels, local(): pl.pallas_call(finish, out_shape=(jax.ShapeDtypeStruct((rows, states), F3...  0.65 us

profile of v2, /device:TPU:0, one launch (start us, length us, event | category | flops | bytes accessed | tf_op | source)
XLA Modules:
  0.0 19.7 jit_solution(112006514353839901)
XLA Ops:
  1.3 17.7 %kalman.1 = (f32[192,128]{1,0:T(8,128)S(1)}, f32[1,128]{1,0:T(1,128)S(1)}, f32[1,128]{1,0:T(1,128)S(1)}) custom-call(s32[3,64]{1,0:T(4,128)} %present_v.1, s32[1]{0:T(128)S(6)} %copy.11.sensors_s, f32[192,128]{1,0:T(8,128)} %bitcast.6, s32[3,64]{1,0:T(4,128)} %present_v.1, f32[1,128]{1,0:T(1,128)} %bitcast.7, f32[128,128]{1,0:T(8,128)} %dyn.1, ...), custom_call_target="tpu_custom_call" | custom-call | tf_op jit(solution)/shard_map/kalman/pallas_call | solution.py:588
  19.0 0.7 %finish.1 = (f32[192,128]{1,0:T(8,128)}, f32[1,128]{1,0:T(1,128)}, f32[1,1]{1,0:T(1,128)}) custom-call(f32[192,128]{1,0:T(8,128)S(1)} %get-tuple-element.9.smoothed, f32[1,128]{1,0:T(1,128)S(1)} %get-tuple-element.10.new_prec, f32[1,128]{1,0:T(1,128)S(1)} %get-tuple-element.11.loglik), custom_call_target="tpu_custom_call" | custom-call | tf_op jit(solution)/shard_map/finish/pallas_call | solution.py:638

commit v3 on v2

--- a/solution.py
+++ b/solution.py
@@ -66,11 +66,11 @@
     present_s, sensors_s, obs, present_v, log_prec, dyn, prior_var, obs_map, init,
     out, new_prec, loglik,
     words, table, theta, theta_4, nodes, vecs, psi_f, psi_n, us, offs, u_rows, u_4, ents, powers, laps, step_rhs,
-    drive, mask, prior, filt, suffix, chunk8,
+    drive, mask, prior, filt, suffix, chunk8, moves, held, pair_2, heads, head_vecs,
     even_node, even_v, pair_node, pair_v, prev_node, prev_v, omega_node, omega_v, psi_own, psi_v, state,
     vec_in, vec_out, vec_back, mat_out, mat_in, comp_out, comp_in, psi_out, psi_in,
-    off_out, off_in, near_out, near_in, sum_buf, sum_in,
-    vec_send, vec_recv, mat_sem, comp_sem, psi_sem, near_sem, off_send, off_recv, sum_send, sum_recv,
+    off_out, off_in, first_in, near_out, near_in, sum_buf, sum_in,
+    vec_send, vec_recv, mat_sem, comp_sem, psi_sem, near_sem, off_send, off_recv, first_sem, sum_send, sum_recv,
 ):
     pos = lax.axis_index("tm")
     par = lax.rem(pos, 2)
@@ -90,6 +90,7 @@
     vec_in[...] = jnp.zeros_like(vec_in)
     off_in[...] = jnp.zeros_like(off_in)
     near_in[...] = jnp.zeros_like(near_in)
+    first_in[...] = jnp.zeros_like(first_in)
     barrier = pltpu.get_barrier_semaphore()
     for d in range(1, n):
         pl.semaphore_signal(barrier, inc=1, device_id={"tm": lax.rem(pos + d, n)}, device_id_type=MESH)
@@ -107,8 +108,12 @@
     d_2n = split(d_mat)
     d_t2 = split(d_t)
     readout = wide(d_t2, deep(split(h_mat.T)))[0]
-    f_t = d_t - mul(readout * weight_on, h_2) * pv
-    f_t2 = split(f_t)
+    gain = -(mul(readout * weight_on, h_2) * pv)
+    f_t2 = split(d_t + gain)
+    held[0] = d_2n
+    held[4] = d_t2
+    held[5] = split(gain)
+    held[6] = split(readout)
 
     for b in range(seqs):
         for k in range(chunks):
@@ -124,12 +129,15 @@
 
     drive[...] = mul(obs[...] * weight_on, h_2) * pv * mask[...]
 
-    step_rhs[...] = stacked(jnp.concatenate([d_t, f_t], axis=1))
+    step_rhs[...] = stacked(jnp.concatenate([d_t, gain], axis=1))
     singles = [d_t2, f_t2]
     both = deep(jnp.concatenate(singles, axis=1))
     pairs = []
     for a in range(2):
         pairs += [split(q) for q in wide(singles[a], both)]
+    for a in range(4):
+        pair_2[a] = pairs[a]
+    held[7] = f_t2
     quad_rhs = deep(jnp.concatenate(pairs, axis=1))
     for a in range(4):
         quad = wide(pairs[a], quad_rhs)
@@ -141,12 +149,19 @@
 
     def advance(x, i):
         y = times(x, step_rhs[...])
-        return jnp.where(at(mask, i) > 0.5, y[:, states:], y[:, :states]) + at(drive, i)
-
-    zero_states = [at(drive, 0)]
+        move = jnp.where(at(mask, i) > 0.5, y[:, states:], 0.0) + at(drive, i)
+        return y[:, :states] + move, move
+
+    x = at(drive, 0)
+    moves[0:total, :] = x
     for i in range(1, WORD):
-        zero_states.append(advance(zero_states[-1], i))
-    offs[...] = zero_states[-1]
+        x, move = advance(x, i)
+        moves[i * total : (i + 1) * total, :] = move
+    offs[...] = x
+
+    def combine(moved, first):
+        left = jnp.concatenate([twice(stacked(moved[j * total : (j + 1) * total, :])) for j in range(first + 1, WORD)], axis=1)
+        return product(left, jnp.concatenate([tall(held[j]) for j in range(WORD - 1 - first)], axis=0))
 
     def leading(matrix, v):
         return jnp.concatenate([matrix, split(jnp.broadcast_to(v, (16, states)))], axis=0)
@@ -211,7 +226,7 @@
     comp = send_mat(comp_out, comp_in, comp_sem, 2)
     psi = send_mat(psi_out, psi_in, psi_sem, 1)
     near = send_mat(near_out, near_in, near_sem, -1)
-    to_next = [send_vec(vec_out, k, shift(by)) for k, by in enumerate((1, 2, 4))]
+    to_next = [send_vec(vec_out, k, shift(by)) for k, by in enumerate((2, 4, 1))]
     to_back = send_vec(vec_back, 3, shift(-1))
 
     even = par == 0
@@ -232,43 +247,47 @@
     def _():
         vec_in[0:seqs, :] = init[...]
         vec_out[...] = apply(lefts(vec_in[...]), own, own_v())
-        to_next[0].start()
-
-    eye = (
-        lax.broadcasted_iota(jnp.int32, (states, states), 0)
-        == lax.broadcasted_iota(jnp.int32, (states, states), 1)
-    ).astype(F32)
-    residual = eye - mul(d_t, d_2n)
-    r_1, d_2 = [mul(a, d_2n) for a in (residual, d_mat)]
-    d_2s = split(d_2)
-    r_2, r_3, d_3, d_4 = [mul(a, d_2s) for a in (residual, r_1, d_mat, d_2)]
-    d_4s = split(d_4)
-    tails = [split(a) for a in (residual, r_1, r_2, r_3)]
-    powers[0] = split(eye)
-    powers[1] = d_4s
-    left = jnp.concatenate([twice(stacked(z)) for z in zero_states], axis=1)
-    u = product(left, jnp.concatenate([tall(a) for a in tails], axis=0))
-    u_rows[...] = u
-    u_4[...] = times(u, tall(d_4s))
-    theta_2 = []
-    for a in range(4):
-        left = jnp.concatenate([singles[a // 2], pairs[a]], axis=1)
-        rhs = jnp.concatenate([deep(tails[0]), deep(tails[1])], axis=0)
-        theta_2.append(wide(left, rhs)[0])
-    theta_rhs = deep(jnp.concatenate([split(mul(a, d_2s)) for a in theta_2], axis=1))
-    for a in range(4):
-        full = wide(pairs[a], theta_rhs)
-        for c in range(4):
-            whole = theta_2[a] + full[c]
-            theta[a * 4 + c] = whole
-            theta_4[a * 4 + c] = split(mul(whole, d_4s))
+        to_next[2].start()
+
+    near_4 = pos < 4
+    far = pos >= 4
+
+    base = held[0]
+    held[1] = mul_node(base, base)
+    square = held[1]
+    held[2] = mul_node(base, square)
+    held[3] = mul_node(square, square)
+    powers[1] = held[3]
 
     @pl.when(pos == 1)
     def _():
         to_back.wait_recv()
         vec_out[...] = apply(lefts(vec_in[...]), own, own_v())
         to_next[0].start()
-        to_next[1].start()
+        to_next[2].start()
+
+    @pl.when(far)
+    def _():
+        fourth = held[3]
+        u = moves[0:total, :] + combine(moves, 0)
+        u_rows[...] = u
+        u_4[...] = times(u, tall(fourth))
+        gain = held[5]
+        whole = gain[:, :states].astype(F32) + gain[:, states:].astype(F32)
+        rhs = deep(mul_node(gain, held[0]))
+        theta_2 = [None, wide(held[4], rhs)[0], whole, whole + wide(held[7], rhs)[0]]
+        rhs = deep(held[1])
+        rhs = deep(jnp.concatenate([split(wide(split(a), rhs)[0]) for a in theta_2[1:]], axis=1))
+        theta[0] = jnp.zeros_like(whole)
+        theta_4[0] = split(jnp.zeros_like(whole))
+        for a in range(4):
+            full = [None] + wide(pair_2[a], rhs)
+            for c in range(4):
+                if a + c > 0:
+                    parts = [q for q in (theta_2[a], full[c]) if q is not None]
+                    whole = sum(parts[1:], parts[0])
+                    theta[a * 4 + c] = whole
+                    theta_4[a * 4 + c] = split(mul(whole, fourth))
 
     @pl.when(has_mat)
     def _():
@@ -288,6 +307,26 @@
     def _():
         comp.start()
 
+    def double(level):
+        half = 1 << (level - 1)
+        powers[2 * half] = mul_node(powers[half], powers[half])
+
+    def fill():
+        powers[0] = split(
+            (
+                lax.broadcasted_iota(jnp.int32, (states, states), 0)
+                == lax.broadcasted_iota(jnp.int32, (states, states), 1)
+            ).astype(F32)
+        )
+        for level in range(1, levels):
+            base = powers[1 << level]
+            for e in range(1, 1 << level):
+                powers[(1 << level) + e] = mul_node(powers[e], base)
+        laps[0] = powers[0]
+        laps[1] = powers[chunks]
+        for m in range(2, 2 * chips - 2):
+            laps[m] = mul_node(laps[m // 2], laps[m - m // 2])
+
     @pl.when(pos == 3)
     def _():
         to_back.wait_recv()
@@ -298,65 +337,73 @@
             for copy in to_next:
                 copy.start()
 
-    for level in range(1, levels + 1):
-        lag = powers[1 << (level - 1)]
-        for j in range(total >> level):
-            left, v_left = child(level, 2 * j)
-            lead = leading(left, v_left)
-            a, b = 2 * j, 2 * j + 1
-            if level == 1:
-                y = wide(lead, deep(theta_4[words[b]]))[0]
-                whole = theta[words[a]] + y[:states]
-                u = y[states : states + EXTRA] + u_4[b : b + 1, :] + u_rows[a : a + 1, :]
-            else:
-                a, b = first[level - 1] + a, first[level - 1] + b
-                y = wide(lead, deep(psi_n[b]))[0]
-                y = jnp.concatenate([y[:states], y[states:] + us[b : b + 1, :]], axis=0)
-                y = mul(y, lag)
-                whole = psi_f[a] + y[:states]
-                u = y[states : states + EXTRA] + us[a : a + 1, :]
-            k = first[level] + j
-            if level == levels:
-                psi_out[j * block : j * block + states, :] = whole
-                psi_out[j * block + states : (j + 1) * block, :] = u
-            else:
-                us[k : k + 1, :] = u[0:1]
-                if j % 2 == 0:
-                    psi_f[k] = whole
+    @pl.when(near_4)
+    def _():
+        for level in range(1, levels + 1):
+            double(level)
+        fill()
+
+    def prepare():
+        for b in range(seqs):
+            for level in range(levels, 0, -1):
+                for p in range(chunks >> level):
+                    mat_2, v = child(level, (b * (chunks >> level) + p) * 2)
+                    k = (p << level) + (1 << (level - 1))
+                    if p > 0:
+                        before = b * chunks + (p << level)
+                        lead = leading(heads[before], head_vecs[before : before + 1, :])
+                        y = wide(lead, deep(mat_2))[0]
+                        mat_2 = split(y[:states])
+                        v = y[states : states + 1] + v
+                    heads[b * chunks + k] = mat_2
+                    head_vecs[b * chunks + k : b * chunks + k + 1, :] = v
+
+    @pl.when(far)
+    def _():
+        for level in range(1, levels + 1):
+            lag = powers[1 << (level - 1)]
+            double(level)
+            for j in range(total >> level):
+                left, v_left = child(level, 2 * j)
+                lead = leading(left, v_left)
+                a, b = 2 * j, 2 * j + 1
+                if level == 1:
+                    y = wide(lead, deep(theta_4[words[b]]))[0]
+                    whole = theta[words[a]] + y[:states]
+                    u = y[states : states + EXTRA] + u_4[b : b + 1, :] + u_rows[a : a + 1, :]
                 else:
-                    psi_n[k] = split(whole)
-        if level < levels:
-            base = powers[1 << (level - 1)]
-            for e in range(1, (1 << (level - 1)) + 1):
-                made = mul_node(powers[e], base)
-                powers[(1 << (level - 1)) + e] = made
-    base = powers[chunks // 2]
-    for e in range(1, chunks // 2 + 1):
-        powers[chunks // 2 + e] = mul_node(powers[e], base)
-    lap = powers[chunks]
-    laps[0] = powers[0]
-    laps[1] = lap
-    for m in range(2, 2 * chips - 2):
-        laps[m] = mul_node(laps[m // 2], laps[m - m // 2])
-
-    @pl.when(gives_mat)
+                    a, b = first[level - 1] + a, first[level - 1] + b
+                    y = wide(lead, deep(psi_n[b]))[0]
+                    y = jnp.concatenate([y[:states], y[states:] + us[b : b + 1, :]], axis=0)
+                    y = mul(y, lag)
+                    whole = psi_f[a] + y[:states]
+                    u = y[states : states + EXTRA] + us[a : a + 1, :]
+                k = first[level] + j
+                if level == levels:
+                    psi_out[j * block : j * block + states, :] = whole
+                    psi_out[j * block + states : (j + 1) * block, :] = u
+                else:
+                    us[k : k + 1, :] = u[0:1]
+                    if j % 2 == 0:
+                        psi_f[k] = whole
+                    else:
+                        psi_n[k] = split(whole)
+
+    @pl.when(jnp.logical_and(gives_mat, far))
     def _():
         psi.start()
 
-    @pl.when(pos == n - 1)
-    def _():
-        close = split(mul(d_t, lap))
-        for b in range(seqs):
-            y = wide(leading(nodes[top + b], vecs[top + b : top + b + 1, :]), deep(close))[0]
-            psi_out[b * block : (b + 1) * block, :] += y[:block]
-
-    for b in range(seqs):
-        psi_own[b] = split(psi_out[b * block : b * block + states, :])
-    psi_v[...] = rows_of(psi_out)
-
-    @pl.when(has_mat)
+    @pl.when(far)
+    def _():
+        for b in range(seqs):
+            psi_own[b] = split(psi_out[b * block : b * block + states, :])
+        psi_v[...] = rows_of(psi_out)
+        fill()
+
+    @pl.when(jnp.logical_and(odd, far))
     def _():
         parts = []
+        lap = powers[chunks]
         for b in range(seqs):
             v_left = mat_in[b * block + states : b * block + states + 1, :]
             y = wide(leading(even_node[b], v_left), deep(psi_own[b]))[0]
@@ -369,6 +416,14 @@
             omega_node[b] = split(psi_in[b * block : b * block + states, :])
         omega_v[...] = rows_of(psi_in)
 
+    direct = jnp.logical_and(odd, far)
+
+    headed = jnp.logical_and(even, far)
+
+    @pl.when(headed)
+    def _():
+        prepare()
+
     def send_off(d, side):
         return pltpu.make_async_remote_copy(
             src_ref=off_out, dst_ref=off_in.at[d - 1], send_sem=off_send.at[2 * d - 2 + side], recv_sem=off_recv.at[d - 1],
@@ -400,58 +455,55 @@
         for copy in to_next:
             copy.start()
 
-    @pl.when(has_mat)
+    @pl.when(jnp.logical_and(odd, far))
     def _():
         left = lefts(state[...])
         off_out[...] = apply(left, omega_node, omega_v[...])
-        for d in range(1, chips):
+        for d in range(chips - 1, 0, -1):
             @pl.when(chip - d >= 0)
             def _(d=d):
                 send_off(d, 1).start()
                 send_off(d, 0).start()
-        state[...] = apply(left, even_node, even_v[...])
-
-    @pl.when(odd)
-    def _():
-        near_out[...] = apply(lefts(state[...]), psi_own, psi_v[...])
+        x = apply(left, even_node, even_v[...])
+        state[...] = x
+        near_out[...] = apply(lefts(x), psi_own, psi_v[...])
         near.start()
 
-    x = state[...]
-    entering = []
-    for b in range(seqs):
-        entering.append(jnp.broadcast_to(x[b : b + 1], (8, states)))
-    for level in range(levels, 0, -1):
-        below = []
-        for j in range(total >> level):
-            node, v = child(level, 2 * j)
-            below.append(entering[j])
-            below.append(times(entering[j], tall(node)) + v)
-        entering = below
-    for j in range(total):
-        ents[j : j + 1, :] = entering[j][0:1]
+    @pl.when(pos == 3)
+    def _():
+        state[...] = apply(lefts(state[...]), even_node, even_v[...])
+
+    @pl.when(headed)
+    def _():
+        x = state[...]
+        spread = jnp.concatenate([jnp.concatenate([tall(heads[b * chunks + k]) for k in range(1, chunks)], axis=1) for b in range(seqs)], axis=0)
+        y = product(lefts(x), spread)
+        for b in range(seqs):
+            ents[b * chunks : b * chunks + 1, :] = x[b : b + 1]
+            for k in range(1, chunks):
+                r = b * chunks + k
+                ents[r : r + 1, :] = y[b : b + 1, (k - 1) * states : k * states] + head_vecs[r : r + 1, :]
+
+    @pl.when(jnp.logical_not(headed))
+    def _():
+        x = state[...]
+        entering = [jnp.broadcast_to(x[b : b + 1], (8, states)) for b in range(seqs)]
+        for level in range(levels, 0, -1):
+            below = []
+            for j in range(total >> level):
+                node, v = child(level, 2 * j)
+                below.append(entering[j])
+                below.append(times(entering[j], tall(node)) + v)
+            entering = below
+        for j in range(total):
+            ents[j : j + 1, :] = entering[j][0:1]
 
     x = ents[...]
     for i in range(WORD):
         prior[i * total : (i + 1) * total, :] = x
-        x = advance(x, i)
+        x, move = advance(x, i)
         filt[i * total : (i + 1) * total, :] = x
-
-    chunk8[...] = jnp.zeros_like(chunk8)
-    for i in range(WORD):
-        left = jnp.concatenate([twice(stacked(filt[j * total : (j + 1) * total, :])) for j in range(i, WORD)], axis=1)
-        z = product(left, jnp.concatenate([tall(tails[j]) for j in range(WORD - i)], axis=0))
-        suffix[i * total : (i + 1) * total, :] = z
-        if i == 0:
-            for b in range(seqs):
-                chunk8[pl.ds(b, chunks, stride=8), :] = z[b * chunks : (b + 1) * chunks]
-    ends = chunk8[...].reshape(chunks, 8, states)
-
-    errors = jnp.concatenate([at(obs, i) for i in range(WORD)], axis=0) - mul(prior[...], split(readout))
-    seen = jnp.concatenate([at(mask, i) for i in range(WORD)], axis=0)
-    squares = jnp.sum(seen * active * errors * errors, axis=0, keepdims=True)
-    number = jnp.sum(seen, axis=0, keepdims=True)
-    sums = jnp.where(row8 == 0, jnp.broadcast_to(squares, (8, states)), jnp.broadcast_to(number, (8, states)))
-    sum_buf[...] = sums
+        moves[i * total : (i + 1) * total, :] = move
 
     def send_sum(d):
         return pltpu.make_async_remote_copy(
@@ -459,14 +511,40 @@
             device_id={"tm": lax.rem(pos + d + 1, n)}, device_id_type=MESH,
         )
 
-    for d in range(n - 1):
-        send_sum(d).start()
-
-    last = jnp.zeros((8, states), F32)
-    for b in range(seqs):
-        r = (WORD - 1) * total + (b + 1) * chunks - 1
-        last = jnp.where(row8 == b, jnp.broadcast_to(filt[r : r + 1, :], (8, states)), last)
-    final = times(last, tall(d_t2))
+    def score():
+        errors = jnp.concatenate([at(obs, i) for i in range(WORD)], axis=0) - mul(prior[...], held[6])
+        seen = jnp.concatenate([at(mask, i) for i in range(WORD)], axis=0)
+        squares = jnp.sum(seen * active * errors * errors, axis=0, keepdims=True)
+        number = jnp.sum(seen, axis=0, keepdims=True)
+        sums = jnp.where(row8 == 0, jnp.broadcast_to(squares, (8, states)), jnp.broadcast_to(number, (8, states)))
+        sum_buf[...] = sums
+        for e in range(1, n):
+            d = e - 1
+            @pl.when(pos + e >= n)
+            def _(d=d):
+                send_sum(d).start()
+
+        for e in range(n - 1, 0, -1):
+            d = e - 1
+            @pl.when(pos + e < n)
+            def _(d=d):
+                send_sum(d).start()
+
+    @pl.when(far)
+    def _():
+        score()
+
+    chunk8[...] = jnp.zeros_like(chunk8)
+    for i in range(WORD - 1):
+        z = combine(moves, i)
+        suffix[i * total : (i + 1) * total, :] = filt[i * total : (i + 1) * total, :] + z
+        if i == 0:
+            z = z + moves[0:total, :]
+            for b in range(seqs):
+                chunk8[pl.ds(b, chunks, stride=8), :] = z[b * chunks : (b + 1) * chunks]
+    i = WORD - 1
+    suffix[i * total : (i + 1) * total, :] = filt[i * total : (i + 1) * total, :]
+    ends = chunk8[...].reshape(chunks, 8, states)
 
     ups = [ends]
     for level in range(levels):
@@ -474,6 +552,31 @@
         half = pair.shape[0]
         later = times(pair[:, 1].reshape(half * 8, states), tall(powers[1 << level]))
         ups.append(pair[:, 0] + later.reshape(half, 8, states))
+
+    def send_first(slot, side):
+        dst = off_in.at[0] if slot == 0 else first_in
+        return pltpu.make_async_remote_copy(
+            src_ref=off_out, dst_ref=dst, send_sem=off_send.at[side],
+            recv_sem=off_recv.at[0] if slot == 0 else first_sem,
+            device_id={"tm": side}, device_id_type=MESH,
+        )
+
+    @pl.when(near_4)
+    def _():
+        off_out[...] = ups[-1].reshape(8, states)
+        near_out[...] = ups[-1].reshape(8, states)
+        for slot in range(2):
+            @pl.when(pos == 2 + slot)
+            def _(slot=slot):
+                send_first(slot, 0).start()
+                send_first(slot, 1).start()
+
+        @pl.when(odd)
+        def _():
+            near.start()
+
+        score()
+
     x = jnp.zeros((1, 8, states), F32)
     for level in range(levels - 1, -1, -1):
         count = x.shape[0]
@@ -490,24 +593,29 @@
     def _():
         near.wait_recv()
 
+    @pl.when(chip == 0)
+    def _():
+        send_first(1, 0).wait_recv()
+
     for d in range(1, chips):
         @pl.when(chip + d < chips)
         def _(d=d):
             send_off(d, 0).wait_recv()
 
-    left = jnp.concatenate([twice(stacked(off_in[d])) for d in range(chips - 1)], axis=1)
-    rhs = jnp.concatenate([tall(laps[2 * d + 1 - par]) for d in range(chips - 1)], axis=0)
-    x = jnp.where(pos == n - 1, final, near_in[...] + product(left, rhs))
+    left = jnp.concatenate([twice(stacked(a)) for a in [first_in[...]] + [off_in[d] for d in range(chips - 1)]], axis=1)
+    rhs = jnp.concatenate([tall(laps[2 - par])] + [tall(laps[2 * d + 1 - par]) for d in range(chips - 1)], axis=0)
+    x = near_in[...] + product(left, rhs)
     y = times(x, jnp.concatenate([tall(powers[chunks - 1 - k]) for k in range(chunks)], axis=1))
     for k in range(chunks):
         chunk8[k * 8 : (k + 1) * 8, :] += y[:, k * states : (k + 1) * states]
     x = jnp.concatenate([chunk8[pl.ds(b, chunks, stride=8), :] for b in range(seqs)], axis=0)
-    y = times(x, jnp.concatenate([tall(a) for a in (d_4s, split(d_3), d_2s, d_2n)], axis=1))
+    y = times(x, jnp.concatenate([tall(a) for a in (held[3], held[2], held[1], held[0])], axis=1))
     for i in range(WORD):
         out[pl.ds(i, total, stride=WORD), :] = (
             suffix[i * total : (i + 1) * total, :] + y[:, i * states : (i + 1) * states]
         )
 
+    sums = sum_buf[...]
     for d in range(n - 1):
         send_sum(d).wait_recv()
         sums = sums + sum_in[d]
@@ -520,6 +628,9 @@
     @pl.when(gives_mat)
     def _():
         mat.wait_send()
+
+    @pl.when(jnp.logical_and(gives_mat, far))
+    def _():
         psi.wait_send()
 
     @pl.when(gives_comp)
@@ -528,12 +639,12 @@
 
     @pl.when(pos == 0)
     def _():
+        to_next[2].wait_send()
+
+    @pl.when(pos == 1)
+    def _():
         to_next[0].wait_send()
-
-    @pl.when(pos == 1)
-    def _():
-        to_next[0].wait_send()
-        to_next[1].wait_send()
+        to_next[2].wait_send()
 
     @pl.when(last_of_four)
     def _():
@@ -549,10 +660,16 @@
         near.wait_send()
 
     for d in range(1, chips):
-        @pl.when(jnp.logical_and(has_mat, chip - d >= 0))
+        @pl.when(jnp.logical_and(jnp.logical_and(odd, far), chip - d >= 0))
         def _(d=d):
             send_off(d, 0).wait_send()
             send_off(d, 1).wait_send()
+
+    for slot in range(2):
+        @pl.when(pos == 2 + slot)
+        def _(slot=slot):
+            send_first(slot, 0).wait_send()
+            send_first(slot, 1).wait_send()
 
     for d in range(n - 1):
         send_sum(d).wait_send()
@@ -617,6 +734,11 @@
             pltpu.VMEM((rows, states), F32),
             pltpu.VMEM((rows, states), F32),
             pltpu.VMEM((chunks * 8, states), F32),
+            pltpu.VMEM((rows, states), F32),
+            pltpu.VMEM((8,) + node, BF16),
+            pltpu.VMEM((4,) + node, BF16),
+            pltpu.VMEM((total,) + node, BF16),
+            pltpu.VMEM((total, states), F32),
             pltpu.VMEM((seqs,) + node, BF16), tile,
             pltpu.VMEM((seqs,) + node, BF16), tile,
             pltpu.VMEM((seqs,) + node, BF16), tile,
@@ -624,9 +746,9 @@
             pltpu.VMEM((seqs,) + node, BF16), tile,
             tile,
             tile, tile, tile, whole, whole, whole, whole, whole, whole,
-            tile, pltpu.VMEM((chips - 1, 8, states), F32), tile, tile, tile, pltpu.VMEM((n, 8, states), F32),
+            tile, pltpu.VMEM((chips - 1, 8, states), F32), tile, tile, tile, tile, pltpu.VMEM((n, 8, states), F32),
             dma((4,)), dma(()), dma((2,)), dma((2,)), dma((2,)), dma((2,)),
-            dma((2 * chips - 2,)), dma((chips - 1,)), dma((n,)), dma((n,)),
+            dma((2 * chips - 2,)), dma((chips - 1,)), dma(()), dma((n,)), dma((n,)),
         ],
         compiler_params=pltpu.CompilerParams(collective_id=0, has_side_effects=True),
         name="kalman",

time: 19.8 us -> 18.9 us (0.955)
  Pallas kernels: 18.4 us -> 17.5 us
    pallas_call x1, Pallas kernels: 17.7 us -> 16.8 us  [local(): pl.pallas_call(functools.partial(kernel, n, seqs, steps), out_shape=(pltp...]
where the time goes in v3:
time: 18.9 us; the launch traced here: 18.8 us
  Pallas kernels  17.5 us (93%)
  between operations  1.29 us (7%)
    pallas_call x1, Pallas kernels, local(): pl.pallas_call(functools.partial(kernel, n, seqs, steps), out_shape=(pltp...  16.8 us
    pallas_call x1, Pallas kernels, local(): pl.pallas_call(finish, out_shape=(jax.ShapeDtypeStruct((rows, states), F3...  0.65 us

profile of v3, /device:TPU:0, one launch (start us, length us, event | category | flops | bytes accessed | tf_op | source)
XLA Modules:
  0.0 18.8 jit_solution(13924467550090397712)
XLA Ops:
  1.3 16.8 %kalman.1 = (f32[192,128]{1,0:T(8,128)S(1)}, f32[1,128]{1,0:T(1,128)S(1)}, f32[1,128]{1,0:T(1,128)S(1)}) custom-call(s32[3,64]{1,0:T(4,128)} %present_v.1, s32[1]{0:T(128)S(6)} %copy.11.sensors_s, f32[192,128]{1,0:T(8,128)} %bitcast.6, s32[3,64]{1,0:T(4,128)} %present_v.1, f32[1,128]{1,0:T(1,128)} %bitcast.7, f32[128,128]{1,0:T(8,128)} %dyn.1, ...), custom_call_target="tpu_custom_call" | custom-call | tf_op jit(solution)/shard_map/kalman/pallas_call | solution.py:705
  18.1 0.7 %finish.1 = (f32[192,128]{1,0:T(8,128)}, f32[1,128]{1,0:T(1,128)}, f32[1,1]{1,0:T(1,128)}) custom-call(f32[192,128]{1,0:T(8,128)S(1)} %get-tuple-element.9.smoothed, f32[1,128]{1,0:T(1,128)S(1)} %get-tuple-element.10.new_prec, f32[1,128]{1,0:T(1,128)S(1)} %get-tuple-element.11.loglik), custom_call_target="tpu_custom_call" | custom-call | tf_op jit(solution)/shard_map/finish/pallas_call | solution.py:760

commit v4 on v3

--- a/solution.py
+++ b/solution.py
@@ -66,11 +66,11 @@
     present_s, sensors_s, obs, present_v, log_prec, dyn, prior_var, obs_map, init,
     out, new_prec, loglik,
     words, table, theta, theta_4, nodes, vecs, psi_f, psi_n, us, offs, u_rows, u_4, ents, powers, laps, step_rhs,
-    drive, mask, prior, filt, suffix, chunk8, moves, held, pair_2, heads, head_vecs,
+    drive, mask, prior, filt, suffix, chunk8, moves, held, pair_2, zero_2, theta_2, theta_d, later, heads, head_vecs,
     even_node, even_v, pair_node, pair_v, prev_node, prev_v, omega_node, omega_v, psi_own, psi_v, state,
     vec_in, vec_out, vec_back, mat_out, mat_in, comp_out, comp_in, psi_out, psi_in,
     off_out, off_in, first_in, near_out, near_in, sum_buf, sum_in,
-    vec_send, vec_recv, mat_sem, comp_sem, psi_sem, near_sem, off_send, off_recv, first_sem, sum_send, sum_recv,
+    vec_send, vec_recv, mat_sem, comp_sem, psi_sem, near_sem, off_send, off_recv, first_sem, sum_sem,
 ):
     pos = lax.axis_index("tm")
     par = lax.rem(pos, 2)
@@ -157,6 +157,8 @@
     for i in range(1, WORD):
         x, move = advance(x, i)
         moves[i * total : (i + 1) * total, :] = move
+        if i == 1:
+            zero_2[...] = x
     offs[...] = x
 
     def combine(moved, first):
@@ -209,7 +211,7 @@
 
     def send_vec(src, slot, to):
         return pltpu.make_async_remote_copy(
-            src_ref=src, dst_ref=vec_in, send_sem=vec_send.at[slot], recv_sem=vec_recv,
+            src_ref=src, dst_ref=vec_in, send_sem=vec_send.at[slot // 3], recv_sem=vec_recv,
             device_id={"tm": to}, device_id_type=MESH,
         )
 
@@ -222,8 +224,18 @@
             device_id={"tm": shift(by)}, device_id_type=MESH,
         )
 
-    mat = send_mat(mat_out, mat_in, mat_sem, 1)
-    comp = send_mat(comp_out, comp_in, comp_sem, 2)
+    def arrived(ref, sem):
+        pltpu.make_async_copy(ref, ref, sem).wait()
+
+    def send_part(src, dst, sem, by, b):
+        rows = pl.ds(b * block, block)
+        return pltpu.make_async_remote_copy(
+            src_ref=src.at[rows], dst_ref=dst.at[rows], send_sem=sem.at[0], recv_sem=sem.at[1 + (b if by == 1 else 0)],
+            device_id={"tm": shift(by)}, device_id_type=MESH,
+        )
+
+    mats = [send_part(mat_out, mat_in, mat_sem, 1, b) for b in range(seqs)]
+    comps = [send_part(comp_out, comp_in, comp_sem, 2, b) for b in range(seqs)]
     psi = send_mat(psi_out, psi_in, psi_sem, 1)
     near = send_mat(near_out, near_in, near_sem, -1)
     to_next = [send_vec(vec_out, k, shift(by)) for k, by in enumerate((2, 4, 1))]
@@ -241,7 +253,8 @@
 
     @pl.when(gives_mat)
     def _():
-        mat.start()
+        for copy in mats:
+            copy.start()
 
     @pl.when(pos == 0)
     def _():
@@ -258,6 +271,13 @@
     held[2] = mul_node(base, square)
     held[3] = mul_node(square, square)
     powers[1] = held[3]
+    rhs = deep(mul_node(held[5], base))
+    change = held[5]
+    change = change[:, :states].astype(F32) + change[:, states:].astype(F32)
+    parts = [wide(held[4], rhs)[0], change, change + wide(held[7], rhs)[0]]
+    for a in range(3):
+        theta_2[a] = parts[a]
+        theta_d[:, 2 * a * states : 2 * (a + 1) * states] = split(mul(parts[a], square))
 
     @pl.when(pos == 1)
     def _():
@@ -266,46 +286,58 @@
         to_next[0].start()
         to_next[2].start()
 
-    @pl.when(far)
-    def _():
+    def pair(b):
+        left = split(mat_in[b * block : b * block + states, :])
+        even_node[b] = left
+        v_left = mat_in[b * block + states : b * block + states + 1, :]
+        y = wide(leading(left, v_left), deep(nodes[top + b]))[0]
+        pair_node[b] = split(y[:states])
+        comp_out[b * block : b * block + states, :] = y[:states]
+        comp_out[b * block + states : (b + 1) * block, :] = y[states : states + EXTRA] + vecs[top + b : top + b + 1, :]
+
+    def tables():
         fourth = held[3]
         u = moves[0:total, :] + combine(moves, 0)
         u_rows[...] = u
         u_4[...] = times(u, tall(fourth))
-        gain = held[5]
-        whole = gain[:, :states].astype(F32) + gain[:, states:].astype(F32)
-        rhs = deep(mul_node(gain, held[0]))
-        theta_2 = [None, wide(held[4], rhs)[0], whole, whole + wide(held[7], rhs)[0]]
-        rhs = deep(held[1])
-        rhs = deep(jnp.concatenate([split(wide(split(a), rhs)[0]) for a in theta_2[1:]], axis=1))
+        rhs = deep(theta_d[...])
+        whole = jnp.zeros((states, states), F32)
         theta[0] = jnp.zeros_like(whole)
         theta_4[0] = split(jnp.zeros_like(whole))
         for a in range(4):
             full = [None] + wide(pair_2[a], rhs)
             for c in range(4):
                 if a + c > 0:
-                    parts = [q for q in (theta_2[a], full[c]) if q is not None]
+                    parts = [q for q in (theta_2[a - 1] if a > 0 else None, full[c]) if q is not None]
                     whole = sum(parts[1:], parts[0])
                     theta[a * 4 + c] = whole
                     theta_4[a * 4 + c] = split(mul(whole, fourth))
 
-    @pl.when(has_mat)
-    def _():
-        mat.wait_recv()
+    @pl.when(jnp.logical_and(far, jnp.logical_not(gives_comp)))
+    def _():
+        tables()
+
+    @pl.when(gives_comp)
+    def _():
+        for b in range(seqs):
+            mats[b].wait_recv()
+            pair(b)
+            comps[b].start()
         even_v[...] = rows_of(mat_in)
-        for b in range(seqs):
-            left = split(mat_in[b * block : b * block + states, :])
-            even_node[b] = left
-            v_left = mat_in[b * block + states : b * block + states + 1, :]
-            y = wide(leading(left, v_left), deep(nodes[top + b]))[0]
-            pair_node[b] = split(y[:states])
-            comp_out[b * block : b * block + states, :] = y[:states]
-            comp_out[b * block + states : (b + 1) * block, :] = y[states : states + EXTRA] + vecs[top + b : top + b + 1, :]
         pair_v[...] = rows_of(comp_out)
 
     @pl.when(gives_comp)
     def _():
-        comp.start()
+        tables()
+
+    @pl.when(jnp.logical_and(has_mat, jnp.logical_not(gives_comp)))
+    def _():
+        for b in range(seqs):
+            mats[b].wait_recv()
+        for b in range(seqs):
+            pair(b)
+        even_v[...] = rows_of(mat_in)
+        pair_v[...] = rows_of(comp_out)
 
     def double(level):
         half = 1 << (level - 1)
@@ -341,7 +373,6 @@
     def _():
         for level in range(1, levels + 1):
             double(level)
-        fill()
 
     def prepare():
         for b in range(seqs):
@@ -398,23 +429,16 @@
         for b in range(seqs):
             psi_own[b] = split(psi_out[b * block : b * block + states, :])
         psi_v[...] = rows_of(psi_out)
-        fill()
 
     @pl.when(jnp.logical_and(odd, far))
     def _():
-        parts = []
         lap = powers[chunks]
         for b in range(seqs):
             v_left = mat_in[b * block + states : b * block + states + 1, :]
             y = wide(leading(even_node[b], v_left), deep(psi_own[b]))[0]
             u = psi_out[b * block + states : b * block + states + 1, :]
             y = jnp.concatenate([y[:states], y[states:] + u], axis=0)
-            parts.append(mul(y, lap)[:block])
-        psi.wait_recv()
-        for b in range(seqs):
-            psi_in[b * block : (b + 1) * block, :] += parts[b]
-            omega_node[b] = split(psi_in[b * block : b * block + states, :])
-        omega_v[...] = rows_of(psi_in)
+            later[b * block : (b + 1) * block, :] = mul(y, lap)[:block]
 
     direct = jnp.logical_and(odd, far)
 
@@ -426,24 +450,33 @@
 
     def send_off(d, side):
         return pltpu.make_async_remote_copy(
-            src_ref=off_out, dst_ref=off_in.at[d - 1], send_sem=off_send.at[2 * d - 2 + side], recv_sem=off_recv.at[d - 1],
+            src_ref=off_out, dst_ref=off_in.at[d - 1], send_sem=off_send.at[d - 1], recv_sem=off_recv.at[d - 1],
             device_id={"tm": lax.rem(2 * (chip + chips - d) + side, n)}, device_id_type=MESH,
         )
 
-    @pl.when(jnp.logical_or(pos == 2, pos >= 4))
+    @pl.when(has_comp)
     def _():
         to_back.wait_recv()
-
-    @pl.when(has_comp)
-    def _():
-        comp.wait_recv()
+        arrived(comp_in, comp_sem.at[1])
+        for b in range(seqs):
+            prev_node[b] = split(comp_in[b * block : b * block + states, :])
         prev_v[...] = rows_of(comp_in)
-        for b in range(seqs):
-            prev_node[b] = split(comp_in[b * block : b * block + states, :])
         back = apply(lefts(vec_in[...]), prev_node, prev_v[...])
         vec_back[...] = back
         to_back.start()
         state[...] = back
+
+    @pl.when(direct)
+    def _():
+        psi.wait_recv()
+        for b in range(seqs):
+            psi_in[b * block : (b + 1) * block, :] += later[b * block : (b + 1) * block, :]
+            omega_node[b] = split(psi_in[b * block : b * block + states, :])
+        omega_v[...] = rows_of(psi_in)
+
+    @pl.when(jnp.logical_and(jnp.logical_or(pos == 2, pos >= 4), jnp.logical_not(has_comp)))
+    def _():
+        to_back.wait_recv()
 
     @pl.when(jnp.logical_not(has_comp))
     def _():
@@ -473,6 +506,35 @@
     def _():
         state[...] = apply(lefts(state[...]), even_node, even_v[...])
 
+    def send_sum(d):
+        return pltpu.make_async_remote_copy(
+            src_ref=sum_buf, dst_ref=sum_in.at[d], send_sem=sum_sem.at[0], recv_sem=sum_sem.at[1],
+            device_id={"tm": lax.rem(pos + d + 1, n)}, device_id_type=MESH,
+        )
+
+    def score(priors):
+        squares = jnp.zeros((total, states), F32)
+        seen = jnp.zeros((total, states), F32)
+        for i in range(WORD):
+            error = at(obs, i) - mul(priors[i], held[6])
+            squares = squares + at(mask, i) * error * error
+            seen = seen + at(mask, i)
+        squares = active * jnp.sum(squares, axis=0, keepdims=True)
+        number = jnp.sum(seen, axis=0, keepdims=True)
+        sum_buf[...] = jnp.where(row8 == 0, jnp.broadcast_to(squares, (8, states)), jnp.broadcast_to(number, (8, states)))
+        for e in range(1, n):
+            @pl.when(pos + e >= n)
+            def _(e=e):
+                send_sum(e - 1).start()
+
+        for e in range(n - 1, 0, -1):
+            @pl.when(pos + e < n)
+            def _(e=e):
+                send_sum(e - 1).start()
+
+    def priors_held():
+        return [prior[i * total : (i + 1) * total, :] for i in range(WORD)]
+
     @pl.when(headed)
     def _():
         x = state[...]
@@ -483,6 +545,13 @@
             for k in range(1, chunks):
                 r = b * chunks + k
                 ents[r : r + 1, :] = y[b : b + 1, (k - 1) * states : k * states] + head_vecs[r : r + 1, :]
+        start = ents[...]
+        y = times(start, jnp.concatenate([step_rhs[...]] + [tall(pair_2[a]) for a in range(4)], axis=1))
+        y = [y[:, k * states : (k + 1) * states] for k in range(6)]
+        on = [at(mask, i) > 0.5 for i in range(2)]
+        one = y[0] + jnp.where(on[0], y[1], 0.0) + at(drive, 0)
+        two = jnp.where(on[0], jnp.where(on[1], y[5], y[4]), jnp.where(on[1], y[3], y[2])) + zero_2[...]
+        score([start, one, two, advance(two, 2)[0]])
 
     @pl.when(jnp.logical_not(headed))
     def _():
@@ -505,34 +574,9 @@
         filt[i * total : (i + 1) * total, :] = x
         moves[i * total : (i + 1) * total, :] = move
 
-    def send_sum(d):
-        return pltpu.make_async_remote_copy(
-            src_ref=sum_buf, dst_ref=sum_in.at[d], send_sem=sum_send.at[d], recv_sem=sum_recv.at[d],
-            device_id={"tm": lax.rem(pos + d + 1, n)}, device_id_type=MESH,
-        )
-
-    def score():
-        errors = jnp.concatenate([at(obs, i) for i in range(WORD)], axis=0) - mul(prior[...], held[6])
-        seen = jnp.concatenate([at(mask, i) for i in range(WORD)], axis=0)
-        squares = jnp.sum(seen * active * errors * errors, axis=0, keepdims=True)
-        number = jnp.sum(seen, axis=0, keepdims=True)
-        sums = jnp.where(row8 == 0, jnp.broadcast_to(squares, (8, states)), jnp.broadcast_to(number, (8, states)))
-        sum_buf[...] = sums
-        for e in range(1, n):
-            d = e - 1
-            @pl.when(pos + e >= n)
-            def _(d=d):
-                send_sum(d).start()
-
-        for e in range(n - 1, 0, -1):
-            d = e - 1
-            @pl.when(pos + e < n)
-            def _(d=d):
-                send_sum(d).start()
-
-    @pl.when(far)
-    def _():
-        score()
+    @pl.when(direct)
+    def _():
+        score(priors_held())
 
     chunk8[...] = jnp.zeros_like(chunk8)
     for i in range(WORD - 1):
@@ -556,7 +600,7 @@
     def send_first(slot, side):
         dst = off_in.at[0] if slot == 0 else first_in
         return pltpu.make_async_remote_copy(
-            src_ref=off_out, dst_ref=dst, send_sem=off_send.at[side],
+            src_ref=off_out, dst_ref=dst, send_sem=off_send.at[0],
             recv_sem=off_recv.at[0] if slot == 0 else first_sem,
             device_id={"tm": side}, device_id_type=MESH,
         )
@@ -575,7 +619,7 @@
         def _():
             near.start()
 
-        score()
+        score(priors_held())
 
     x = jnp.zeros((1, 8, states), F32)
     for level in range(levels - 1, -1, -1):
@@ -588,6 +632,7 @@
             sooner = moved.reshape(count, 8, states) + pair[:, 1]
         x = jnp.stack([sooner, x], axis=1).reshape(2 * count, 8, states)
     chunk8[...] = x.reshape(chunks * 8, states)
+    fill()
 
     @pl.when(even)
     def _():
@@ -615,9 +660,9 @@
             suffix[i * total : (i + 1) * total, :] + y[:, i * states : (i + 1) * states]
         )
 
+    arrived(sum_in.at[pl.ds(0, n - 1)], sum_sem.at[1])
     sums = sum_buf[...]
     for d in range(n - 1):
-        send_sum(d).wait_recv()
         sums = sums + sum_in[d]
     squares, number = sums[0:1], sums[1:2]
     grad = 0.5 * active * (number - weight * squares)
@@ -627,7 +672,7 @@
 
     @pl.when(gives_mat)
     def _():
-        mat.wait_send()
+        arrived(mat_out, mat_sem.at[0])
 
     @pl.when(jnp.logical_and(gives_mat, far))
     def _():
@@ -635,7 +680,7 @@
 
     @pl.when(gives_comp)
     def _():
-        comp.wait_send()
+        arrived(comp_out, comp_sem.at[0])
 
     @pl.when(pos == 0)
     def _():
@@ -643,13 +688,11 @@
 
     @pl.when(pos == 1)
     def _():
-        to_next[0].wait_send()
-        to_next[2].wait_send()
+        arrived(off_in.at[pl.ds(0, 2)], vec_send.at[0])
 
     @pl.when(last_of_four)
     def _():
-        for copy in to_next:
-            copy.wait_send()
+        arrived(off_in.at[pl.ds(0, 3)], vec_send.at[0])
 
     @pl.when(has_comp)
     def _():
@@ -662,17 +705,14 @@
     for d in range(1, chips):
         @pl.when(jnp.logical_and(jnp.logical_and(odd, far), chip - d >= 0))
         def _(d=d):
-            send_off(d, 0).wait_send()
-            send_off(d, 1).wait_send()
+            arrived(off_in.at[pl.ds(0, 2)], off_send.at[d - 1])
 
     for slot in range(2):
         @pl.when(pos == 2 + slot)
         def _(slot=slot):
-            send_first(slot, 0).wait_send()
-            send_first(slot, 1).wait_send()
-
-    for d in range(n - 1):
-        send_sum(d).wait_send()
+            arrived(off_in.at[pl.ds(0, 2)], off_send.at[0])
+
+    arrived(sum_in.at[pl.ds(0, n - 1)], sum_sem.at[0])
 
 
 def mul_node(left, right):
@@ -737,6 +777,10 @@
             pltpu.VMEM((rows, states), F32),
             pltpu.VMEM((8,) + node, BF16),
             pltpu.VMEM((4,) + node, BF16),
+            pltpu.VMEM((total, states), F32),
+            pltpu.VMEM((3, states, states), F32),
+            pltpu.VMEM((states, 6 * states), BF16),
+            whole,
             pltpu.VMEM((total,) + node, BF16),
             pltpu.VMEM((total, states), F32),
             pltpu.VMEM((seqs,) + node, BF16), tile,
@@ -747,8 +791,8 @@
             tile,
             tile, tile, tile, whole, whole, whole, whole, whole, whole,
             tile, pltpu.VMEM((chips - 1, 8, states), F32), tile, tile, tile, tile, pltpu.VMEM((n, 8, states), F32),
-            dma((4,)), dma(()), dma((2,)), dma((2,)), dma((2,)), dma((2,)),
-            dma((2 * chips - 2,)), dma((chips - 1,)), dma(()), dma((n,)), dma((n,)),
+            dma((2,)), dma(()), dma((1 + seqs,)), dma((2,)), dma((2,)), dma((2,)),
+            dma((chips - 1,)), dma((chips - 1,)), dma(()), dma((2,)),
         ],
         compiler_params=pltpu.CompilerParams(collective_id=0, has_side_effects=True),
         name="kalman",

time: 18.9 us -> 18 us (0.952)
  Pallas kernels: 17.5 us -> 16.6 us
    pallas_call x1, Pallas kernels: 16.8 us -> 15.9 us  [local(): pl.pallas_call(functools.partial(kernel, n, seqs, steps), out_shape=(pltp...]
where the time goes in v4:
time: 18 us; the launch traced here: 17.9 us
  Pallas kernels  16.6 us (92%)
  between operations  1.29 us (7%)
    pallas_call x1, Pallas kernels, local(): pl.pallas_call(functools.partial(kernel, n, seqs, steps), out_shape=(pltp...  15.9 us
    pallas_call x1, Pallas kernels, local(): pl.pallas_call(finish, out_shape=(jax.ShapeDtypeStruct((rows, states), F3...  0.65 us

profile of v4, /device:TPU:0, one launch (start us, length us, event | category | flops | bytes accessed | tf_op | source)
XLA Modules:
  0.0 17.9 jit_solution(7933292236537824946)
XLA Ops:
  1.3 15.9 %kalman.1 = (f32[192,128]{1,0:T(8,128)S(1)}, f32[1,128]{1,0:T(1,128)S(1)}, f32[1,128]{1,0:T(1,128)S(1)}) custom-call(s32[3,64]{1,0:T(4,128)} %present_v.1, s32[1]{0:T(128)S(6)} %copy.11.sensors_s, f32[192,128]{1,0:T(8,128)} %bitcast.6, s32[3,64]{1,0:T(4,128)} %present_v.1, f32[1,128]{1,0:T(1,128)} %bitcast.7, f32[128,128]{1,0:T(8,128)} %dyn.1, ...), custom_call_target="tpu_custom_call" | custom-call | tf_op jit(solution)/shard_map/kalman/pallas_call | solution.py:745
  17.2 0.7 %finish.1 = (f32[192,128]{1,0:T(8,128)}, f32[1,128]{1,0:T(1,128)}, f32[1,1]{1,0:T(1,128)}) custom-call(f32[192,128]{1,0:T(8,128)S(1)} %get-tuple-element.9.smoothed, f32[1,128]{1,0:T(1,128)S(1)} %get-tuple-element.10.new_prec, f32[1,128]{1,0:T(1,128)S(1)} %get-tuple-element.11.loglik), custom_call_target="tpu_custom_call" | custom-call | tf_op jit(solution)/shard_map/finish/pallas_call | solution.py:804

commit v5 on v4

--- a/solution.py
+++ b/solution.py
@@ -68,9 +68,9 @@
     words, table, theta, theta_4, nodes, vecs, psi_f, psi_n, us, offs, u_rows, u_4, ents, powers, laps, step_rhs,
     drive, mask, prior, filt, suffix, chunk8, moves, held, pair_2, zero_2, theta_2, theta_d, later, heads, head_vecs,
     even_node, even_v, pair_node, pair_v, prev_node, prev_v, omega_node, omega_v, psi_own, psi_v, state,
-    vec_in, vec_out, vec_back, mat_out, mat_in, comp_out, comp_in, psi_out, psi_in,
+    vec_in, vec_out, vec_back, mat_out, mat_in, comp_out, comp_in, early_in, psi_out, psi_in,
     off_out, off_in, first_in, near_out, near_in, sum_buf, sum_in,
-    vec_send, vec_recv, mat_sem, comp_sem, psi_sem, near_sem, off_send, off_recv, first_sem, sum_sem,
+    vec_send, vec_recv, mat_sem, early_sem, comp_sem, psi_sem, near_sem, off_send, off_recv, first_sem, sum_sem,
 ):
     pos = lax.axis_index("tm")
     par = lax.rem(pos, 2)
@@ -234,8 +234,17 @@
             device_id={"tm": shift(by)}, device_id_type=MESH,
         )
 
+    def send_early(slot, by):
+        return pltpu.make_async_remote_copy(
+            src_ref=mat_out.at[pl.ds(0, block)], dst_ref=early_in.at[pl.ds(slot * block, block)],
+            send_sem=early_sem.at[0], recv_sem=early_sem.at[1 + slot],
+            device_id={"tm": shift(by)}, device_id_type=MESH,
+        )
+
+    early = [send_early(0, 3), send_early(1, 2)]
+    order = list(range(1, seqs)) + [0]
     mats = [send_part(mat_out, mat_in, mat_sem, 1, b) for b in range(seqs)]
-    comps = [send_part(comp_out, comp_in, comp_sem, 2, b) for b in range(seqs)]
+    comps = [None] + [send_part(comp_out, comp_in, comp_sem, 2, b) for b in range(1, seqs)]
     psi = send_mat(psi_out, psi_in, psi_sem, 1)
     near = send_mat(near_out, near_in, near_sem, -1)
     to_next = [send_vec(vec_out, k, shift(by)) for k, by in enumerate((2, 4, 1))]
@@ -253,8 +262,16 @@
 
     @pl.when(gives_mat)
     def _():
-        for copy in mats:
-            copy.start()
+        for b in order:
+            mats[b].start()
+
+        @pl.when(quarter == 0)
+        def _():
+            early[0].start()
+
+    @pl.when(gives_comp)
+    def _():
+        early[1].start()
 
     @pl.when(pos == 0)
     def _():
@@ -319,12 +336,14 @@
 
     @pl.when(gives_comp)
     def _():
-        for b in range(seqs):
+        for b in order:
             mats[b].wait_recv()
-            pair(b)
-            comps[b].start()
+            if b > 0:
+                pair(b)
+                comps[b].start()
+            else:
+                even_node[b] = split(mat_in[b * block : b * block + states, :])
         even_v[...] = rows_of(mat_in)
-        pair_v[...] = rows_of(comp_out)
 
     @pl.when(gives_comp)
     def _():
@@ -454,10 +473,18 @@
             device_id={"tm": lax.rem(2 * (chip + chips - d) + side, n)}, device_id_type=MESH,
         )
 
+    rest = pl.ds(block, (seqs - 1) * block)
+
     @pl.when(has_comp)
     def _():
+        for copy in early:
+            copy.wait_recv()
+        v_left = early_in[states : states + 1, :]
+        y = wide(leading(split(early_in[0:states, :]), v_left), deep(split(early_in[block : block + states, :])))[0]
+        comp_in[0:states, :] = y[:states]
+        comp_in[states:block, :] = y[states : states + EXTRA] + early_in[block + states : 2 * block, :]
         to_back.wait_recv()
-        arrived(comp_in, comp_sem.at[1])
+        arrived(comp_in.at[rest], comp_sem.at[1])
         for b in range(seqs):
             prev_node[b] = split(comp_in[b * block : b * block + states, :])
         prev_v[...] = rows_of(comp_in)
@@ -532,19 +559,7 @@
             def _(e=e):
                 send_sum(e - 1).start()
 
-    def priors_held():
-        return [prior[i * total : (i + 1) * total, :] for i in range(WORD)]
-
-    @pl.when(headed)
-    def _():
-        x = state[...]
-        spread = jnp.concatenate([jnp.concatenate([tall(heads[b * chunks + k]) for k in range(1, chunks)], axis=1) for b in range(seqs)], axis=0)
-        y = product(lefts(x), spread)
-        for b in range(seqs):
-            ents[b * chunks : b * chunks + 1, :] = x[b : b + 1]
-            for k in range(1, chunks):
-                r = b * chunks + k
-                ents[r : r + 1, :] = y[b : b + 1, (k - 1) * states : k * states] + head_vecs[r : r + 1, :]
+    def quick():
         start = ents[...]
         y = times(start, jnp.concatenate([step_rhs[...]] + [tall(pair_2[a]) for a in range(4)], axis=1))
         y = [y[:, k * states : (k + 1) * states] for k in range(6)]
@@ -552,6 +567,21 @@
         one = y[0] + jnp.where(on[0], y[1], 0.0) + at(drive, 0)
         two = jnp.where(on[0], jnp.where(on[1], y[5], y[4]), jnp.where(on[1], y[3], y[2])) + zero_2[...]
         score([start, one, two, advance(two, 2)[0]])
+
+    def priors_held():
+        return [prior[i * total : (i + 1) * total, :] for i in range(WORD)]
+
+    @pl.when(headed)
+    def _():
+        x = state[...]
+        spread = jnp.concatenate([jnp.concatenate([tall(heads[b * chunks + k]) for k in range(1, chunks)], axis=1) for b in range(seqs)], axis=0)
+        y = product(lefts(x), spread)
+        for b in range(seqs):
+            ents[b * chunks : b * chunks + 1, :] = x[b : b + 1]
+            for k in range(1, chunks):
+                r = b * chunks + k
+                ents[r : r + 1, :] = y[b : b + 1, (k - 1) * states : k * states] + head_vecs[r : r + 1, :]
+        quick()
 
     @pl.when(jnp.logical_not(headed))
     def _():
@@ -567,16 +597,16 @@
         for j in range(total):
             ents[j : j + 1, :] = entering[j][0:1]
 
+        @pl.when(far)
+        def _():
+            quick()
+
     x = ents[...]
     for i in range(WORD):
         prior[i * total : (i + 1) * total, :] = x
         x, move = advance(x, i)
         filt[i * total : (i + 1) * total, :] = x
         moves[i * total : (i + 1) * total, :] = move
-
-    @pl.when(direct)
-    def _():
-        score(priors_held())
 
     chunk8[...] = jnp.zeros_like(chunk8)
     for i in range(WORD - 1):
@@ -674,13 +704,18 @@
     def _():
         arrived(mat_out, mat_sem.at[0])
 
+        @pl.when(quarter == 0)
+        def _():
+            arrived(mat_out.at[pl.ds(0, block)], early_sem.at[0])
+
     @pl.when(jnp.logical_and(gives_mat, far))
     def _():
         psi.wait_send()
 
     @pl.when(gives_comp)
     def _():
-        arrived(comp_out, comp_sem.at[0])
+        arrived(comp_out.at[rest], comp_sem.at[0])
+        arrived(mat_out.at[pl.ds(0, block)], early_sem.at[0])
 
     @pl.when(pos == 0)
     def _():
@@ -789,9 +824,9 @@
             pltpu.VMEM((seqs,) + node, BF16), tile,
             pltpu.VMEM((seqs,) + node, BF16), tile,
             tile,
-            tile, tile, tile, whole, whole, whole, whole, whole, whole,
+            tile, tile, tile, whole, whole, whole, whole, pltpu.VMEM((2 * (states + EXTRA), states), F32), whole, whole,
             tile, pltpu.VMEM((chips - 1, 8, states), F32), tile, tile, tile, tile, pltpu.VMEM((n, 8, states), F32),
-            dma((2,)), dma(()), dma((1 + seqs,)), dma((2,)), dma((2,)), dma((2,)),
+            dma((2,)), dma(()), dma((1 + seqs,)), dma((3,)), dma((2,)), dma((2,)), dma((2,)),
             dma((chips - 1,)), dma((chips - 1,)), dma(()), dma((2,)),
         ],
         compiler_params=pltpu.CompilerParams(collective_id=0, has_side_effects=True),

time: 18 us -> 17.6 us (0.978)
  Pallas kernels: 16.6 us -> 16.2 us
    pallas_call x1, Pallas kernels: 15.9 us -> 15.5 us  [local(): pl.pallas_call(functools.partial(kernel, n, seqs, steps), out_shape=(pltp...]
where the time goes in v5:
time: 17.6 us; the launch traced here: 17.5 us
  Pallas kernels  16.2 us (92%)
  between operations  1.29 us (7%)
    pallas_call x1, Pallas kernels, local(): pl.pallas_call(functools.partial(kernel, n, seqs, steps), out_shape=(pltp...  15.5 us
    pallas_call x1, Pallas kernels, local(): pl.pallas_call(finish, out_shape=(jax.ShapeDtypeStruct((rows, states), F3...  0.65 us

profile of v5, /device:TPU:0, one launch (start us, length us, event | category | flops | bytes accessed | tf_op | source)
XLA Modules:
  0.0 17.5 jit_solution(15931101970580530795)
XLA Ops:
  1.3 15.5 %kalman.1 = (f32[192,128]{1,0:T(8,128)S(1)}, f32[1,128]{1,0:T(1,128)S(1)}, f32[1,128]{1,0:T(1,128)S(1)}) custom-call(s32[3,64]{1,0:T(4,128)} %present_v.1, s32[1]{0:T(128)S(6)} %copy.11.sensors_s, f32[192,128]{1,0:T(8,128)} %bitcast.6, s32[3,64]{1,0:T(4,128)} %present_v.1, f32[1,128]{1,0:T(1,128)} %bitcast.7, f32[128,128]{1,0:T(8,128)} %dyn.1, ...), custom_call_target="tpu_custom_call" | custom-call | tf_op jit(solution)/shard_map/kalman/pallas_call | solution.py:780
  16.8 0.7 %finish.1 = (f32[192,128]{1,0:T(8,128)}, f32[1,128]{1,0:T(1,128)}, f32[1,1]{1,0:T(1,128)}) custom-call(f32[192,128]{1,0:T(8,128)S(1)} %get-tuple-element.9.smoothed, f32[1,128]{1,0:T(1,128)S(1)} %get-tuple-element.10.new_prec, f32[1,128]{1,0:T(1,128)S(1)} %get-tuple-element.11.loglik), custom_call_target="tpu_custom_call" | custom-call | tf_op jit(solution)/shard_map/finish/pallas_call | solution.py:839

commit v6 on v5

--- a/solution.py
+++ b/solution.py
@@ -63,8 +63,9 @@
 
 def kernel(
     n, seqs, steps,
-    present_s, sensors_s, obs, present_v, log_prec, dyn, prior_var, obs_map, init,
+    present_h, sensors_s, obs_h, log_prec_h, dyn_h, prior_var_h, obs_map_h, init_h,
     out, new_prec, loglik,
+    dyn, obs_map, log_prec, prior_var, present_s, present_v, obs, init, in_sem,
     words, table, theta, theta_4, nodes, vecs, psi_f, psi_n, us, offs, u_rows, u_4, ents, powers, laps, step_rhs,
     drive, mask, prior, filt, suffix, chunk8, moves, held, pair_2, zero_2, theta_2, theta_d, later, heads, head_vecs,
     even_node, even_v, pair_node, pair_v, prev_node, prev_v, omega_node, omega_v, psi_own, psi_v, state,
@@ -87,6 +88,15 @@
         first.append(first[-1] + (total >> (level - 1) if level > 1 else 0))
     top = first[levels]
 
+    loads = [
+        pltpu.make_async_copy(src, dst, in_sem.at[k])
+        for k, (src, dst) in enumerate([
+            (dyn_h, dyn), (obs_map_h, obs_map), (log_prec_h, log_prec), (prior_var_h, prior_var),
+            (present_h, present_s), (present_h, present_v), (obs_h, obs), (init_h, init),
+        ])
+    ]
+    for copy in loads:
+        copy.start()
     vec_in[...] = jnp.zeros_like(vec_in)
     off_in[...] = jnp.zeros_like(off_in)
     near_in[...] = jnp.zeros_like(near_in)
@@ -95,6 +105,8 @@
     for d in range(1, n):
         pl.semaphore_signal(barrier, inc=1, device_id={"tm": lax.rem(pos + d, n)}, device_id_type=MESH)
 
+    for copy in loads[:4]:
+        copy.wait()
     lane = lax.broadcasted_iota(jnp.int32, (1, states), 1)
     row8 = lax.broadcasted_iota(jnp.int32, (8, states), 0)
     active = (lane < sensors_s[0]).astype(F32)
@@ -115,6 +127,8 @@
     held[5] = split(gain)
     held[6] = split(readout)
 
+    for copy in loads[4:]:
+        copy.wait()
     for b in range(seqs):
         for k in range(chunks):
             t = k * WORD
@@ -408,9 +422,8 @@
                     heads[b * chunks + k] = mat_2
                     head_vecs[b * chunks + k : b * chunks + k + 1, :] = v
 
-    @pl.when(far)
-    def _():
-        for level in range(1, levels + 1):
+    def compose(first_level, last_level):
+        for level in range(first_level, last_level + 1):
             lag = powers[1 << (level - 1)]
             double(level)
             for j in range(total >> level):
@@ -439,41 +452,13 @@
                     else:
                         psi_n[k] = split(whole)
 
-    @pl.when(jnp.logical_and(gives_mat, far))
-    def _():
-        psi.start()
-
     @pl.when(far)
     def _():
-        for b in range(seqs):
-            psi_own[b] = split(psi_out[b * block : b * block + states, :])
-        psi_v[...] = rows_of(psi_out)
-
-    @pl.when(jnp.logical_and(odd, far))
-    def _():
-        lap = powers[chunks]
-        for b in range(seqs):
-            v_left = mat_in[b * block + states : b * block + states + 1, :]
-            y = wide(leading(even_node[b], v_left), deep(psi_own[b]))[0]
-            u = psi_out[b * block + states : b * block + states + 1, :]
-            y = jnp.concatenate([y[:states], y[states:] + u], axis=0)
-            later[b * block : (b + 1) * block, :] = mul(y, lap)[:block]
-
-    direct = jnp.logical_and(odd, far)
-
-    headed = jnp.logical_and(even, far)
-
-    @pl.when(headed)
-    def _():
-        prepare()
-
-    def send_off(d, side):
-        return pltpu.make_async_remote_copy(
-            src_ref=off_out, dst_ref=off_in.at[d - 1], send_sem=off_send.at[d - 1], recv_sem=off_recv.at[d - 1],
-            device_id={"tm": lax.rem(2 * (chip + chips - d) + side, n)}, device_id_type=MESH,
-        )
-
-    rest = pl.ds(block, (seqs - 1) * block)
+        compose(1, levels - 1)
+
+    @pl.when(jnp.logical_and(far, jnp.logical_not(has_comp)))
+    def _():
+        compose(levels, levels)
 
     @pl.when(has_comp)
     def _():
@@ -483,6 +468,42 @@
         y = wide(leading(split(early_in[0:states, :]), v_left), deep(split(early_in[block : block + states, :])))[0]
         comp_in[0:states, :] = y[:states]
         comp_in[states:block, :] = y[states : states + EXTRA] + early_in[block + states : 2 * block, :]
+        compose(levels, levels)
+
+    @pl.when(jnp.logical_and(gives_mat, far))
+    def _():
+        psi.start()
+
+    direct = jnp.logical_and(odd, far)
+
+    headed = jnp.logical_and(even, far)
+
+    @pl.when(headed)
+    def _():
+        prepare()
+
+    def send_off(d, side):
+        return pltpu.make_async_remote_copy(
+            src_ref=off_out, dst_ref=off_in.at[d - 1], send_sem=off_send.at[d - 1], recv_sem=off_recv.at[d - 1],
+            device_id={"tm": lax.rem(2 * (chip + chips - d) + side, n)}, device_id_type=MESH,
+        )
+
+    rest = pl.ds(block, (seqs - 1) * block)
+
+    def sweep(x):
+        entering = [jnp.broadcast_to(x[b : b + 1], (8, states)) for b in range(seqs)]
+        for level in range(levels, 0, -1):
+            below = []
+            for j in range(total >> level):
+                node, v = child(level, 2 * j)
+                below.append(entering[j])
+                below.append(times(entering[j], tall(node)) + v)
+            entering = below
+        for j in range(total):
+            ents[j : j + 1, :] = entering[j][0:1]
+
+    @pl.when(has_comp)
+    def _():
         to_back.wait_recv()
         arrived(comp_in.at[rest], comp_sem.at[1])
         for b in range(seqs):
@@ -491,7 +512,26 @@
         back = apply(lefts(vec_in[...]), prev_node, prev_v[...])
         vec_back[...] = back
         to_back.start()
-        state[...] = back
+        vec_in[...] = back
+        x = apply(lefts(back), even_node, even_v[...])
+        state[...] = x
+        sweep(x)
+
+    @pl.when(far)
+    def _():
+        for b in range(seqs):
+            psi_own[b] = split(psi_out[b * block : b * block + states, :])
+        psi_v[...] = rows_of(psi_out)
+
+    @pl.when(jnp.logical_and(odd, far))
+    def _():
+        lap = powers[chunks]
+        for b in range(seqs):
+            v_left = mat_in[b * block + states : b * block + states + 1, :]
+            y = wide(leading(even_node[b], v_left), deep(psi_own[b]))[0]
+            u = psi_out[b * block + states : b * block + states + 1, :]
+            y = jnp.concatenate([y[:states], y[states:] + u], axis=0)
+            later[b * block : (b + 1) * block, :] = mul(y, lap)[:block]
 
     @pl.when(direct)
     def _():
@@ -511,13 +551,13 @@
 
     @pl.when(jnp.logical_and(has_comp, pos < n - 1))
     def _():
-        vec_out[...] = apply(lefts(state[...]), pair_node, pair_v[...])
+        vec_out[...] = apply(lefts(vec_in[...]), pair_node, pair_v[...])
         for copy in to_next:
             copy.start()
 
     @pl.when(jnp.logical_and(odd, far))
     def _():
-        left = lefts(state[...])
+        left = lefts(vec_in[...])
         off_out[...] = apply(left, omega_node, omega_v[...])
         for d in range(chips - 1, 0, -1):
             @pl.when(chip - d >= 0)
@@ -583,23 +623,13 @@
                 ents[r : r + 1, :] = y[b : b + 1, (k - 1) * states : k * states] + head_vecs[r : r + 1, :]
         quick()
 
-    @pl.when(jnp.logical_not(headed))
-    def _():
-        x = state[...]
-        entering = [jnp.broadcast_to(x[b : b + 1], (8, states)) for b in range(seqs)]
-        for level in range(levels, 0, -1):
-            below = []
-            for j in range(total >> level):
-                node, v = child(level, 2 * j)
-                below.append(entering[j])
-                below.append(times(entering[j], tall(node)) + v)
-            entering = below
-        for j in range(total):
-            ents[j : j + 1, :] = entering[j][0:1]
-
-        @pl.when(far)
-        def _():
-            quick()
+    @pl.when(jnp.logical_not(jnp.logical_or(headed, has_comp)))
+    def _():
+        sweep(state[...])
+
+    @pl.when(direct)
+    def _():
+        quick()
 
     x = ents[...]
     for i in range(WORD):
@@ -690,6 +720,55 @@
             suffix[i * total : (i + 1) * total, :] + y[:, i * states : (i + 1) * states]
         )
 
+    @pl.when(gives_mat)
+    def _():
+        arrived(mat_out, mat_sem.at[0])
+
+        @pl.when(quarter == 0)
+        def _():
+            arrived(mat_out.at[pl.ds(0, block)], early_sem.at[0])
+
+    @pl.when(jnp.logical_and(gives_mat, far))
+    def _():
+        psi.wait_send()
+
+    @pl.when(gives_comp)
+    def _():
+        arrived(comp_out.at[rest], comp_sem.at[0])
+        arrived(mat_out.at[pl.ds(0, block)], early_sem.at[0])
+
+    @pl.when(pos == 0)
+    def _():
+        to_next[2].wait_send()
+
+    @pl.when(pos == 1)
+    def _():
+        arrived(off_in.at[pl.ds(0, 2)], vec_send.at[0])
+
+    @pl.when(last_of_four)
+    def _():
+        arrived(off_in.at[pl.ds(0, 3)], vec_send.at[0])
+
+    @pl.when(has_comp)
+    def _():
+        to_back.wait_send()
+
+    @pl.when(odd)
+    def _():
+        near.wait_send()
+
+    for d in range(1, chips):
+        @pl.when(jnp.logical_and(jnp.logical_and(odd, far), chip - d >= 0))
+        def _(d=d):
+            arrived(off_in.at[pl.ds(0, 2)], off_send.at[d - 1])
+
+    for slot in range(2):
+        @pl.when(pos == 2 + slot)
+        def _(slot=slot):
+            arrived(off_in.at[pl.ds(0, 2)], off_send.at[0])
+
+    arrived(sum_in.at[pl.ds(0, n - 1)], sum_sem.at[0])
+
     arrived(sum_in.at[pl.ds(0, n - 1)], sum_sem.at[1])
     sums = sum_buf[...]
     for d in range(n - 1):
@@ -699,55 +778,6 @@
     new_prec[...] = log_prec[...] + grad / (seqs * steps * n)
     terms = 0.5 * active * (log_prec[...] * number - weight * squares)
     loglik[...] = jnp.zeros_like(terms) + jnp.sum(terms, axis=1, keepdims=True) / (seqs * steps * n * states)
-
-    @pl.when(gives_mat)
-    def _():
-        arrived(mat_out, mat_sem.at[0])
-
-        @pl.when(quarter == 0)
-        def _():
-            arrived(mat_out.at[pl.ds(0, block)], early_sem.at[0])
-
-    @pl.when(jnp.logical_and(gives_mat, far))
-    def _():
-        psi.wait_send()
-
-    @pl.when(gives_comp)
-    def _():
-        arrived(comp_out.at[rest], comp_sem.at[0])
-        arrived(mat_out.at[pl.ds(0, block)], early_sem.at[0])
-
-    @pl.when(pos == 0)
-    def _():
-        to_next[2].wait_send()
-
-    @pl.when(pos == 1)
-    def _():
-        arrived(off_in.at[pl.ds(0, 2)], vec_send.at[0])
-
-    @pl.when(last_of_four)
-    def _():
-        arrived(off_in.at[pl.ds(0, 3)], vec_send.at[0])
-
-    @pl.when(has_comp)
-    def _():
-        to_back.wait_send()
-
-    @pl.when(odd)
-    def _():
-        near.wait_send()
-
-    for d in range(1, chips):
-        @pl.when(jnp.logical_and(jnp.logical_and(odd, far), chip - d >= 0))
-        def _(d=d):
-            arrived(off_in.at[pl.ds(0, 2)], off_send.at[d - 1])
-
-    for slot in range(2):
-        @pl.when(pos == 2 + slot)
-        def _(slot=slot):
-            arrived(off_in.at[pl.ds(0, 2)], off_send.at[0])
-
-    arrived(sum_in.at[pl.ds(0, n - 1)], sum_sem.at[0])
 
 
 def mul_node(left, right):
@@ -770,6 +800,7 @@
     inner = sum(total >> level for level in range(1, int(math.log2(chunks)) + 1))
     vmem = pl.BlockSpec(memory_space=pltpu.VMEM)
     smem = pl.BlockSpec(memory_space=pltpu.SMEM)
+    hbm = pl.BlockSpec(memory_space=pl.ANY)
     rows = seqs * steps
     block = seqs * (states + EXTRA)
     node = (states, 2 * states)
@@ -784,9 +815,18 @@
             pltpu.VMEM((1, channels), F32),
             pltpu.VMEM((1, channels), F32),
         ),
-        in_specs=[smem, smem] + [vmem] * 7,
+        in_specs=[hbm, smem] + [hbm] * 6,
         out_specs=(vmem, vmem, vmem),
         scratch_shapes=[
+            pltpu.VMEM((states, states), F32),
+            pltpu.VMEM((channels, states), F32),
+            pltpu.VMEM((1, channels), F32),
+            pltpu.VMEM((1, states), F32),
+            pltpu.SMEM((seqs, steps), jnp.int32),
+            pltpu.VMEM((seqs, steps), jnp.int32),
+            pltpu.VMEM((rows, channels), F32),
+            pltpu.VMEM((seqs, states), F32),
+            dma((8,)),
             pltpu.SMEM((total,), jnp.int32),
             pltpu.VMEM((2**WORD,) + node, BF16),
             pltpu.VMEM((2**WORD, states, states), F32),
@@ -832,7 +872,7 @@
         compiler_params=pltpu.CompilerParams(collective_id=0, has_side_effects=True),
         name="kalman",
     )(
-        present, sensors, obs.reshape(rows, channels), present, log_prec.reshape(1, channels),
+        present, sensors, obs.reshape(rows, channels), log_prec.reshape(1, channels),
         dynamics, prior_var.reshape(1, states), obs_map, init_state,
     )
     held = [pltpu.with_memory_space_constraint(a, pltpu.VMEM) for a in (smoothed, new_prec, loglik)]

time: 17.6 us -> 17.3 us (0.983)
  Pallas kernels: 16.2 us -> 15.9 us
    pallas_call x1, Pallas kernels: 15.5 us -> 15.3 us  [local(): pl.pallas_call(functools.partial(kernel, n, seqs, steps), out_shape=(pltp...]
where the time goes in v6:
time: 17.3 us; the launch traced here: 17.2 us
  Pallas kernels  15.9 us (92%)
  between operations  1.29 us (7%)
    pallas_call x1, Pallas kernels, local(): pl.pallas_call(functools.partial(kernel, n, seqs, steps), out_shape=(pltp...  15.3 us
    pallas_call x1, Pallas kernels, local(): pl.pallas_call(finish, out_shape=(jax.ShapeDtypeStruct((rows, states), F3...  0.65 us

profile of v6, /device:TPU:0, one launch (start us, length us, event | category | flops | bytes accessed | tf_op | source)
XLA Modules:
  0.0 17.2 jit_solution(9781234227795545217)
XLA Ops:
  1.3 15.3 %kalman.1 = (f32[192,128]{1,0:T(8,128)S(1)}, f32[1,128]{1,0:T(1,128)S(1)}, f32[1,128]{1,0:T(1,128)S(1)}) custom-call(s32[3,64]{1,0:T(4,128)} %present_h.1, s32[1]{0:T(128)S(6)} %copy.11.sensors_s, f32[192,128]{1,0:T(8,128)} %bitcast.6, f32[1,128]{1,0:T(1,128)} %bitcast.7, f32[128,128]{1,0:T(8,128)} %dyn_h.1, f32[1,128]{1,0:T(1,128)} %bitcast.8, ...), custom_call_target="tpu_custom_call" | custom-call | tf_op jit(solution)/shard_map/kalman/pallas_call | solution.py:811
  16.5 0.7 %finish.1 = (f32[192,128]{1,0:T(8,128)}, f32[1,128]{1,0:T(1,128)}, f32[1,1]{1,0:T(1,128)}) custom-call(f32[192,128]{1,0:T(8,128)S(1)} %get-tuple-element.9.smoothed, f32[1,128]{1,0:T(1,128)S(1)} %get-tuple-element.10.new_prec, f32[1,128]{1,0:T(1,128)S(1)} %get-tuple-element.11.loglik), custom_call_target="tpu_custom_call" | custom-call | tf_op jit(solution)/shard_map/finish/pallas_call | solution.py:879

commit v7 on v6

--- a/solution.py
+++ b/solution.py
@@ -105,7 +105,7 @@
     for d in range(1, n):
         pl.semaphore_signal(barrier, inc=1, device_id={"tm": lax.rem(pos + d, n)}, device_id_type=MESH)
 
-    for copy in loads[:4]:
+    for copy in loads:
         copy.wait()
     lane = lax.broadcasted_iota(jnp.int32, (1, states), 1)
     row8 = lax.broadcasted_iota(jnp.int32, (8, states), 0)
@@ -127,8 +127,6 @@
     held[5] = split(gain)
     held[6] = split(readout)
 
-    for copy in loads[4:]:
-        copy.wait()
     for b in range(seqs):
         for k in range(chunks):
             t = k * WORD

time: 17.3 us -> 17.4 us (level)
  no operation moved by 1% of the time
where the time goes in v7:
time: 17.4 us; the launch traced here: 17.2 us
  Pallas kernels  15.9 us (91%)
  between operations  1.29 us (7%)
    pallas_call x1, Pallas kernels, local(): pl.pallas_call(functools.partial(kernel, n, seqs, steps), out_shape=(pltp...  15.3 us
    pallas_call x1, Pallas kernels, local(): pl.pallas_call(finish, out_shape=(jax.ShapeDtypeStruct((rows, states), F3...  0.65 us

profile of v7, /device:TPU:0, one launch (start us, length us, event | category | flops | bytes accessed | tf_op | source)
XLA Modules:
  0.0 17.2 jit_solution(11372408328632965203)
XLA Ops:
  1.3 15.3 %kalman.1 = (f32[192,128]{1,0:T(8,128)S(1)}, f32[1,128]{1,0:T(1,128)S(1)}, f32[1,128]{1,0:T(1,128)S(1)}) custom-call(s32[3,64]{1,0:T(4,128)} %present_h.1, s32[1]{0:T(128)S(6)} %copy.11.sensors_s, f32[192,128]{1,0:T(8,128)} %bitcast.6, f32[1,128]{1,0:T(1,128)} %bitcast.7, f32[128,128]{1,0:T(8,128)} %dyn_h.1, f32[1,128]{1,0:T(1,128)} %bitcast.8, ...), custom_call_target="tpu_custom_call" | custom-call | tf_op jit(solution)/shard_map/kalman/pallas_call | solution.py:809
  16.6 0.7 %finish.1 = (f32[192,128]{1,0:T(8,128)}, f32[1,128]{1,0:T(1,128)}, f32[1,1]{1,0:T(1,128)}) custom-call(f32[192,128]{1,0:T(8,128)S(1)} %get-tuple-element.9.smoothed, f32[1,128]{1,0:T(1,128)S(1)} %get-tuple-element.10.new_prec, f32[1,128]{1,0:T(1,128)S(1)} %get-tuple-element.11.loglik), custom_call_target="tpu_custom_call" | custom-call | tf_op jit(solution)/shard_map/finish/pallas_call | solution.py:877
